TPU v7x, 32 devices: a whole 2x2x4 slice. The times are simulated.
32 devices in a mesh: gx: 4 (over z), gy: 4 (over x, core), gz: 2 (over y).
Axes of the slice: x: 2, y: 2, z: 4, core: 2. Of those that a mesh axis runs over, the one named last changes fastest.
Arguments:
- source: float32 [64, 32, 512], P('gx', 'gz', 'gy'), may hold values from -0.6 to 0.6
- shift: float32 [1], replicated, may hold values from 1e-05 to 0.0001
Outputs:
- solution: float32 [64, 32, 512], P('gx', 'gz', 'gy')
All inputs are finite; a program needn't handle non-finite values.
Results may differ from a plain program's by a relative error of at most 0.0004.
Values sent between devices are 32-bit elements; how exact they have to be, the bound alone decides.
A program may use at most 64 MiB of HBM per device.

v0:
```python
import functools

import jax
import jax.numpy as jnp
import numpy as np
from jax import lax
from jax.experimental import pallas as pl
from jax.experimental.pallas import tpu as pltpu
from jax.sharding import PartitionSpec as P

LEVELS = 4
DAMPING = 6.0 / 7.0
PRECISE = lax.Precision.HIGHEST
CUBIC = (
    {-2: -5.0 / 128.0, -1: 35.0 / 128.0, 0: 105.0 / 128.0, 1: -7.0 / 128.0},
    {-1: -7.0 / 128.0, 0: 105.0 / 128.0, 1: 35.0 / 128.0, 2: -5.0 / 128.0},
)
LINEAR = ({-1: 0.25, 0: 0.75}, {0: 0.75, 1: 0.25})
NAMES = ("gx", "gy", "gz")
MESH = pl.DeviceIdType.MESH


def basis(count):
    cells = np.arange(count)
    columns, cosines = [], []
    for m in range(count):
        k = (m + 1) // 2
        angle = 2.0 * np.pi * k * cells / count
        column = np.cos(angle) if m % 2 == 1 or m == 0 else np.sin(angle)
        columns.append(column / np.sqrt(np.sum(column**2)))
        cosines.append(np.cos(2.0 * np.pi * k / count))
    return np.stack(columns, axis=1), np.array(cosines, np.float32)


def interpolation(coarse_count, fine_cells, weights):
    matrix = np.zeros((len(fine_cells), coarse_count))
    for row, cell in enumerate(fine_cells):
        for offset, weight in weights[cell % 2].items():
            matrix[row, (cell // 2 + offset) % coarse_count] += weight
    return matrix


def pairs(coarse_count):
    return np.kron(np.eye(coarse_count), np.ones((1, 2)))


def blocked(matrix):
    count = max(1, 128 // matrix.shape[1])
    return np.kron(np.eye(count), matrix)


def constants(block, sizes):
    b0, b1, b2 = block
    m0, m1, m2 = (size // 2 for size in sizes)
    q0, q1, q2 = (size // 4 for size in sizes)
    c0, c1, c2 = (size // 8 for size in sizes)
    table = {}
    table["own_rows"] = np.kron(np.eye(b0 // 2), pairs(b1 // 2))
    lanes = 0.125 * pairs(b2 // 2).T
    table["own_lo"] = np.concatenate([lanes, np.zeros_like(lanes)], axis=1)
    table["own_hi"] = np.concatenate([np.zeros_like(lanes), lanes], axis=1)
    table["down_rows"] = blocked(pairs(q1))
    table["down_lanes"] = 0.125 * pairs(q2).T
    window_lanes = [b2 + j for j in range(b2 // 2)] + [j - b2 for j in range(b2 // 2, 2 * b2)]
    window_rows = [j - 8 for j in range(b1 + 16)]
    for name, weights in (("cubic", CUBIC), ("linear", LINEAR)):
        table[name + "_rows1"] = blocked(interpolation(q1, range(m1), weights))
        table[name + "_lanes1"] = interpolation(q2, range(m2), weights).T
        table[name + "_rows0"] = blocked(interpolation(m1, window_rows, weights))
        table[name + "_lanes0"] = interpolation(m2, window_lanes, weights).T
    (u0, cos0), (u1, cos1), (u2, cos2) = basis(c0), basis(c1), basis(c2)
    table["spectrum_rows"] = np.kron(u0.T @ pairs(c0), u1.T @ pairs(c1))
    table["spectrum_lanes"] = 0.125 * pairs(c2).T @ u2
    for name, weights in (("cubic", CUBIC), ("linear", LINEAR)):
        table[name + "_rows2"] = np.kron(
            interpolation(c0, range(q0), weights) @ u0, interpolation(c1, range(q1), weights) @ u1
        )
        table[name + "_lanes2"] = u2.T @ interpolation(c2, range(q2), weights).T
    two = np.float32(2.0)
    eigen = (
        np.float32(6.0)
        - two * cos0[:, None, None]
        - two * cos1[None, :, None]
        - two * cos2[None, None, :]
    )
    table["eigen"] = (np.float32(0.25 ** (LEVELS - 1)) * eigen).reshape(c0 * c1, c2)
    wide = ("spectrum_rows", "spectrum_lanes", "eigen")
    return {
        name: np.asarray(
            value, np.float32 if name in wide or name.endswith("2") else jnp.bfloat16
        )
        for name, value in table.items()
    }


def dot(a, b):
    return jnp.dot(a, b, precision=PRECISE, preferred_element_type=jnp.float32)


def parts_of(values, pieces):
    parts = []
    for n in range(pieces):
        parts.append(values.astype(jnp.bfloat16))
        if n + 1 < pieces:
            values = values - parts[-1].astype(jnp.float32)
    return parts[::-1]


def right(values, matrix, pieces):
    terms = [
        jnp.dot(part, matrix, preferred_element_type=jnp.float32)
        for part in parts_of(values, pieces)
    ]
    return sum(terms[1:], terms[0])


def left(matrix, values, pieces):
    terms = [
        jnp.dot(matrix, part, preferred_element_type=jnp.float32)
        for part in parts_of(values, pieces)
    ]
    return sum(terms[1:], terms[0])


def around(plane):
    rows, lanes = plane.shape
    total = pltpu.roll(plane, 1, 0) + pltpu.roll(plane, rows - 1, 0)
    return total + (pltpu.roll(plane, 1, 1) + pltpu.roll(plane, lanes - 1, 1))


def around_all(values):
    first = jnp.concatenate([values[1:], values[:1]], axis=0)
    first = first + jnp.concatenate([values[-1:], values[:-1]], axis=0)
    for axis in (1, 2):
        first = first + pltpu.roll(values, 1, axis)
        first = first + pltpu.roll(values, values.shape[axis] - 1, axis)
    return first


def row_blocks(matrix, values, pieces):
    depth = matrix.shape[1]
    return jnp.concatenate(
        [left(matrix, values[i : i + depth], pieces) for i in range(0, values.shape[0], depth)], axis=0
    )


def loop(count, body):
    def step(i, carry):
        body(i)
        return carry

    lax.fori_loop(0, count, step, 0, unroll=4 if count % 4 == 0 else 2)


def close(ref):
    count = ref.shape[0] - 2
    ref[0] = ref[count]
    ref[count + 1] = ref[1]


def defect_plane(v, p, g, weight, diagonal):
    center = v[p]
    beside = v[p - 1] + v[p + 1] + around(center)
    return center, g - (diagonal * center - weight * beside)


def restrict_own(k, summed):
    b_half, rows, lanes = summed.shape
    folded = left(k["own_rows"][...], summed.reshape(b_half * rows, lanes), 3)
    half = folded.shape[0] // 2
    return right(folded[:half], k["own_lo"][...], 3) + right(folded[half:], k["own_hi"][...], 3)


def unpack(gathered, counts, g):
    nx, ny, nz = counts
    x, y, z = (lax.axis_index(name) for name in NAMES)
    half, rows, lanes = gathered.shape[1:]
    low = lax.broadcasted_iota(jnp.int32, (half, rows, lanes), 2) < lanes // 2
    for dx in range(nx):
        for dz in range(nz):
            for pair in range(ny // 2):
                parts = []
                for dy in (2 * pair, 2 * pair + 1):
                    index = (lax.rem(x + dx, nx) * ny + lax.rem(y + dy, ny)) * nz
                    parts.append(gathered[index + lax.rem(z + dz, nz)])
                turned = [pltpu.roll(part, lanes // 2, 2) for part in parts]
                where = (pl.ds(dz * rows, rows), pl.ds(pair * lanes, lanes))
                start = 2 * half * dx
                g[(pl.ds(start, half), *where)] = jnp.where(low, parts[0], turned[1])
                g[(pl.ds(start + half, half), *where)] = jnp.where(low, turned[0], parts[1])


def solve(k, kind, values, shift):
    shape = values.shape
    flat = values.reshape(shape[0] * shape[1], shape[2])
    spectrum = dot(k["spectrum_rows"][...], dot(flat, k["spectrum_lanes"][...]))
    spectrum = spectrum / (k["eigen"][...] + shift)
    fine = dot(k[kind + "_rows2"][...], dot(spectrum, k[kind + "_lanes2"][...]))
    return fine.reshape(shape)


def cycle2(k, v, g, shift):
    weight = 0.25**2
    diagonal = 6.0 * weight + shift
    damp = DAMPING / diagonal
    if v is None:
        v = damp * g
    else:
        v = v + damp * (g - (diagonal * v - weight * around_all(v)))
    v = v + solve(k, "linear", g - (diagonal * v - weight * around_all(v)), shift)
    return v + damp * (g - (diagonal * v - weight * around_all(v)))


def down(k, t, shape2):
    flat = row_blocks(k["down_rows"][...], t[...].reshape(-1, t.shape[2]), 3)
    return right(flat, k["down_lanes"][...], 3).reshape(shape2)


def up(k, kind, level, values, z):
    flat = right(values, k[kind + "_lanes" + level][...], 2)
    z[...] = row_blocks(k[kind + "_rows" + level][...], flat, 2).reshape(z.shape)


def blend(z, i, weights, count):
    total = None
    for offset, weight in weights.items():
        index = i + offset
        index = index if count is None else lax.rem(index + count, count)
        term = weight * z[index]
        total = term if total is None else total + term
    return total


def up1(k, kind, values, z, v, add):
    count = z.shape[0]
    up(k, kind, "1", values.reshape(-1, values.shape[2]), z)
    weights = CUBIC if kind == "cubic" else LINEAR

    def body(i):
        for odd in (0, 1):
            p = 2 * i + odd + 1
            value = blend(z, i, weights[odd], count)
            v[p] = v[p] + value if add else value

    loop(count, body)
    close(v)


def cycle1(k, v, u, g, t, z, shift, zero, shape2):
    weight = 0.25
    diagonal = 6.0 * weight + shift
    damp = DAMPING / diagonal
    count = g.shape[0]

    def before(p):
        if zero:
            u[p + 1] = damp * g[p]
        else:
            center, rest = defect_plane(v, p + 1, g[p], weight, diagonal)
            u[p + 1] = center + damp * rest

    loop(count, before)
    close(u)

    def residue(i):
        t[i] = (
            defect_plane(u, 2 * i + 1, g[2 * i], weight, diagonal)[1]
            + defect_plane(u, 2 * i + 2, g[2 * i + 1], weight, diagonal)[1]
        )

    loop(count // 2, residue)
    correction = cycle2(k, None, down(k, t, shape2), shift)
    up1(k, "linear", correction, z, u, True)

    def after(p):
        center, rest = defect_plane(u, p + 1, g[p], weight, diagonal)
        v[p + 1] = center + damp * rest

    loop(count, after)
    close(v)


def window(k, kind, v, zw, span, write):
    count = v.shape[0] - 2
    values = jnp.concatenate([v[count - 3 : count + 1], v[1 : span - 3]], axis=0)
    up(k, kind, "0", values.reshape(-1, values.shape[2]), zw)
    weights = CUBIC if kind == "cubic" else LINEAR

    def body(i):
        for odd in (0, 1):
            write(2 * i + odd, blend(zw, i + 3, weights[odd], None))

    loop(span - 6, body)


def own_defect(v, p, f, weight, diagonal):
    rows, lanes = f.shape
    inside = (pl.ds(8, rows), pl.ds(lanes, lanes))
    wide = v[p + 1, pl.ds(8, rows), :]
    center = wide[:, lanes:]
    beside = v[(p, *inside)] + v[(p + 2, *inside)]
    beside = beside + v[p + 1, pl.ds(7, rows), pl.ds(lanes, lanes)]
    beside = beside + v[p + 1, pl.ds(9, rows), pl.ds(lanes, lanes)]
    beside = beside + pltpu.roll(wide, 1, 1)[:, lanes:]
    beside = beside + pltpu.roll(wide, 2 * lanes - 1, 1)[:, lanes:]
    return center, f - (diagonal * center - weight * beside)


def position():
    return tuple(lax.axis_index(name) for name in NAMES)


def partner_of(place):
    x, y, z = place
    return (x, y + 1 - 2 * lax.rem(y, 2), z)


def shifted(place, counts, offset):
    return tuple(
        lax.rem(at + step + count, count) for at, step, count in zip(place, offset, counts)
    )


def slot(place, counts):
    return (place[0] * counts[1] + place[1]) * counts[2] + place[2]


def chip_offsets(counts):
    nx, ny, nz = counts
    offsets = [
        (dx, dy, dz) for dx in range(nx) for dy in range(0, ny, 2) for dz in range(nz)
    ]

    def hops(offset):
        return sum(min(step, count - step) for step, count in zip(offset, (nx, ny, nz)))

    return sorted(offsets[1:], key=hops, reverse=True)


def face_offsets(counts):
    faces = []
    for axis in range(3):
        for side, step in ((0, -1), (1, 1)):
            offset = [0, 0, 0]
            offset[axis] = step
            faces.append((tuple(offset), axis, side))
    return faces


def greet(barrier, places):
    for place in places:
        pl.semaphore_signal(barrier, inc=1, device_id=place, device_id_type=MESH)


def remote(src, dst, send, recv, place):
    return pltpu.make_async_remote_copy(
        src_ref=src, dst_ref=dst, send_sem=send, recv_sem=recv, device_id=place, device_id_type=MESH
    )


def spread(counts, block, gathered, sems):
    send, recv, relay_send, relay_recv = sems
    me = position()
    partner = partner_of(me)
    along, across = stages(counts)
    number = {offset: n for n, offset in enumerate(chip_offsets(counts))}
    mine = gathered.at[slot(me, counts)]
    copies, relays = {}, []

    def pass_on(offset, source, target, place):
        n = number[offset]
        copies[offset] = remote(source, target, send.at[n], recv.at[n], place)
        copies[offset].start()

    def relay(n, source, target):
        relays.append(remote(source, target, relay_send.at[n], relay_recv.at[n], partner))
        relays[-1].start()

    for offset in along + across:
        pass_on(offset, block, mine, shifted(me, counts, offset))
    relay(len(number), block, mine)

    def arrival(offset):
        copies[offset].wait_recv()
        source = shifted(me, counts, tuple(-step for step in offset))
        return gathered.at[slot(source, counts)]

    def finish():
        gathered[slot(me, counts)] = block[...]
        for first in along[::-1]:
            arrived = arrival(first)
            for second in across:
                place = shifted(me, counts, second)
                pass_on((first[0], second[1], second[2]), arrived, arrived, place)
            relay(number[first], arrived, arrived)
        for first in ((0, 0, 0), *along[::-1]):
            for second in across[::-1]:
                offset = (first[0], second[1], second[2])
                arrived = arrival(offset)
                relay(number[offset], arrived, arrived)
        for copy in copies.values():
            copy.wait_send()
        for copy in relays:
            copy.wait()

    return finish


def stages(counts):
    offsets = chip_offsets(counts)
    along = [offset for offset in offsets if offset[1:] == (0, 0)]
    across = [offset for offset in offsets if offset[0] == 0]
    return along, across


def gather_places(counts):
    me = position()
    along, across = stages(counts)
    return [shifted(me, counts, offset) for offset in along + across] + [partner_of(me)]


def first_part(k, counts, source, f, gathered, halos, block, owns, sems, face_sems):
    own_planes, own_rows, own_columns = owns
    planes, rows, columns = halos
    face_send, face_recv = face_sems
    me = position()
    barrier = pltpu.get_barrier_semaphore()
    faces = face_offsets(counts)
    places = gather_places(counts) + [shifted(me, counts, offset) for offset, _, _ in faces]
    greet(barrier, places)
    b0, b1, b2 = source.shape
    summed = source[...].reshape(b0 // 2, 2, b1, b2)
    block[...] = restrict_own(k, summed[:, 0] + summed[:, 1]).reshape(block.shape)
    own_planes[0] = source[0]
    own_planes[1] = source[b0 - 1]
    own_rows[0] = source[:, pl.ds(0, 1), :]
    own_rows[1] = source[:, pl.ds(b1 - 1, 1), :]
    turned = source[...].reshape(b0 * b1, b2).T
    own_columns[0] = turned[:8]
    own_columns[1] = turned[b2 - 8 :]
    pl.semaphore_wait(barrier, len(places))
    finish = spread(counts, block, gathered, sems)
    buffers = ((own_planes, planes), (own_rows, rows), (own_columns, columns))
    order = (0, 2, 1)
    copies = []
    for n, (offset, axis, side) in enumerate(faces):
        own, halo = buffers[order[axis]]
        place = shifted(me, counts, offset)
        copies.append(
            remote(own.at[side], halo.at[1 - side], face_send.at[n], face_recv.at[n], place)
        )
        copies[-1].start()
    f[...] = jnp.zeros_like(f)
    f[1 : b0 + 1, pl.ds(8, b1), pl.ds(b2, b2)] = source[...]
    finish()
    for copy in copies:
        copy.wait()


def second_part(k, counts, shape2, span, shift, gathered, source, halos, out, buffers):
    g, v, u, t, z, zw, v0, v1, f, summed = buffers
    plane_halo, row_halo, column_halo = halos
    unpack(gathered, counts, g)
    b0, b1, b2 = source.shape
    rows, lanes = pl.ds(8, b1), pl.ds(b2, b2)
    f[0, rows, lanes] = plane_halo[0]
    f[b0 + 1, rows, lanes] = plane_halo[1]
    f[1 : b0 + 1, pl.ds(7, 1), lanes] = row_halo[0]
    f[1 : b0 + 1, pl.ds(8 + b1, 1), lanes] = row_halo[1]
    middle = jnp.zeros((b2 - 16, b0 * b1), jnp.float32)
    turned = jnp.concatenate([column_halo[1], middle, column_halo[0]], axis=0)
    f[1 : b0 + 1, rows, pl.ds(0, b2)] = turned.T.reshape(b0, b1, b2)
    def pair_sum(i):
        t[i] = g[2 * i] + g[2 * i + 1]

    loop(g.shape[0] // 2, pair_sum)
    forcing2 = down(k, t, shape2)
    iterate2 = cycle2(k, solve(k, "cubic", forcing2, shift), forcing2, shift)
    up1(k, "cubic", iterate2, z, v, False)
    cycle1(k, v, u, g, t, z, shift, False, shape2)

    def put(p, value):
        v0[p] = value

    window(k, "cubic", v, zw, span, put)
    diagonal = 6.0 + shift
    damp = DAMPING / diagonal

    def before(p):
        center, rest = defect_plane(v0, p + 1, f[p], 1.0, diagonal)
        v1[p] = center + damp * rest

    loop(b0 + 2, before)

    def residue(i):
        summed[i] = (
            own_defect(v1, 2 * i, source[2 * i], 1.0, diagonal)[1]
            + own_defect(v1, 2 * i + 1, source[2 * i + 1], 1.0, diagonal)[1]
        )

    loop(b0 // 2, residue)
    out[...] = restrict_own(k, summed[...]).reshape(out.shape)


def third_part(k, counts, shape2, span, shift, gathered, source, out, buffers):
    g, v, u, t, z, zw, w, v1 = buffers[:8]
    unpack(gathered, counts, g)
    cycle1(k, v, u, g, t, z, shift, True, shape2)
    b0 = source.shape[0]

    def put(p, value):
        w[p] = value

    window(k, "linear", v, zw, span, put)

    def add(p):
        w[p] = v1[p] + w[p + 1]

    loop(b0 + 2, add)
    diagonal = 6.0 + shift
    damp = DAMPING / diagonal

    def after(p):
        center, rest = own_defect(w, p, source[p], 1.0, diagonal)
        out[p] = center + damp * rest

    loop(b0, after)


def kernel(names, counts, shape2, span, *refs):
    k = dict(zip(names, refs))
    shift_ref, source, out, *rest = refs[len(names) :]
    shift = shift_ref[0]
    landing, later, *halos = rest[:5]
    block, block_later, *owns = rest[5:10]
    buffers = rest[10:20]
    sems, sems_later, face_sems = rest[20:24], rest[24:28], rest[28:30]
    f = buffers[8]
    first_part(k, counts, source, f, landing, halos, block, owns, sems, face_sems)
    second_part(k, counts, shape2, span, shift, landing, source, halos, block_later, buffers)
    spread(counts, block_later, later, sems_later)()
    third_part(k, counts, shape2, span, shift, later, source, out, buffers)


def per_device(counts, source, shift):
    nx, ny, nz = counts
    b0, b1, b2 = source.shape
    sizes = (b0 * nx, b1 * nz, b2 * ny)
    table = constants(source.shape, sizes)
    m0, m1, m2 = (size // 2 for size in sizes)
    shape2 = tuple(size // 4 for size in sizes)
    span = b0 // 2 + 8
    wide = (b1 + 16, 2 * b2)
    packed = (b0 // 4, b1 // 2, b2)
    devices = nx * ny * nz
    chips = devices // 2
    vmem = pl.BlockSpec(memory_space=pltpu.VMEM)

    def field(*shape):
        return pltpu.VMEM(shape, jnp.float32)

    faces = [field(2, b1, b2), field(2, b0, 1, b2), field(2, 8, b0 * b1)]
    buffers = [
        field(m0, m1, m2),
        field(m0 + 2, m1, m2),
        field(m0 + 2, m1, m2),
        field(m0 // 2, m1, m2),
        field(m0 // 2, m1, m2),
        field(span, *wide),
        field(b0 + 4, *wide),
        field(b0 + 2, *wide),
        field(b0 + 2, *wide),
        field(b0 // 2, b1, b2),
    ]
    sems = [pltpu.SemaphoreType.DMA((max(chips - 1, 1),))] * 2
    sems += [pltpu.SemaphoreType.DMA((chips,))] * 2
    landing = [field(devices, *packed)] * 2 + faces
    names = tuple(table)
    return pl.pallas_call(
        functools.partial(kernel, names, counts, shape2, span),
        out_shape=jax.ShapeDtypeStruct(source.shape, jnp.float32),
        in_specs=[vmem] * len(names) + [pl.BlockSpec(memory_space=pltpu.SMEM), vmem],
        out_specs=vmem,
        scratch_shapes=landing
        + [field(*packed)] * 2
        + faces
        + buffers
        + sems * 2
        + [pltpu.SemaphoreType.DMA((6,))] * 2,
        compiler_params=pltpu.CompilerParams(
            vmem_limit_bytes=60 * 1024 * 1024, collective_id=0, has_side_effects=True
        ),
    )(*[jnp.asarray(table[name]) for name in names], shift, source)


def solution(mesh):
    counts = tuple(mesh.shape[name] for name in NAMES)
    return jax.shard_map(
        functools.partial(per_device, counts),
        mesh=mesh,
        in_specs=(P("gx", "gz", "gy"), P()),
        out_specs=P("gx", "gz", "gy"),
        check_vma=False,
    )
```

profile of v0, /device:TPU:0, one launch (start us, length us, event | category | flops | bytes accessed | tf_op | source)
XLA Modules:
  0.0 42.7 jit_solution(17750925807923673722)
XLA Ops:
  0.7 40.5 %shard_map.208 = f32[16,16,128]{2,1,0:T(8,128)} custom-call(bf16[64,128]{1,0:T(8,128)(2,1)} %constant.38.clone.refs_0_.refs_3_, bf16[128,128]{1,0:T(8,128)(2,1)} %constant.39.clone.refs_1_, bf16[128,128]{1,0:T(8,128)(2,1)} %constant.40.clone.refs_2_, bf16[64,128]{1,0:T(8,128)(2,1)} %constant.38.clone.refs_0_.refs_3_, ...), custom_call_target="tpu_custom_call" | custom-call | tf_op jit(solution)/shard_map/pallas_call | solution.py:579
  41.1 1.6 %copy.25 = f32[16,16,128]{2,1,0:T(8,128)} copy(f32[16,16,128]{2,1,0:T(8,128)} %shard_map.208) | data formatting | bytes 262144
where the time goes:
time: 42.9 us; the launch traced here: 42.7 us
  Pallas kernels  40.5 us (94%)
  local copies, waits for them, and re-layouts  1.57 us (4%)
  between operations  0.66 us (2%)
    pallas_call x1, Pallas kernels, per_device(): pl.pallas_call(functools.partial(kernel, names, counts, shape2, span), ou...  40.5 us
    unnamed x1, local copies, waits for them, and re-layouts  1.57 us

commit v1 on v0

--- a/solution.py
+++ b/solution.py
@@ -593,10 +593,589 @@
     )(*[jnp.asarray(table[name]) for name in names], shift, source)
 
 
+def modes(count, depth):
+    if depth == 0:
+        return [(0, k) for k in range(count // 2)] + [(1, k) for k in range(1, count // 2 + 1)]
+    half = count // 2
+    low = modes(half, depth - 1)
+    high = []
+    for kind, k in low:
+        if kind == 0:
+            high.append((0, half - k if k else half // 2))
+        else:
+            high.append((1, half - k if k < half // 2 else half))
+    return low + high
+
+
+def waves(count, order):
+    cells = (np.arange(count) + 0.5) * (2.0 * np.pi / count)
+    return np.stack([np.sin(k * cells) if kind else np.cos(k * cells) for kind, k in order], axis=1)
+
+
+def analysis(waves_):
+    return waves_.T / np.sum(waves_**2, axis=0)[:, None]
+
+
+def two_blocks(matrix, axis):
+    first, second = np.split(matrix, 2, axis=axis)
+    return np.concatenate([np.diag(first), np.diag(second)])
+
+
+def factors(m):
+    orders = modes(m, 2), modes(m // 2, 1), modes(m // 4, 0)
+    bases = [waves(len(order), order) for order in orders]
+    t = {"waves": bases[0]}
+    for level, fine, coarse in (("1", bases[0], bases[1]), ("2", bases[1], bases[2])):
+        n = fine.shape[0]
+        t["r" + level] = two_blocks(analysis(coarse) @ (0.5 * pairs(n // 2)) @ fine, 1)
+        for name, weights in (("p", LINEAR), ("q", CUBIC)):
+            matrix = interpolation(n // 2, range(n), weights)
+            t[name + level] = two_blocks(analysis(fine) @ matrix @ coarse, 0)
+        order = orders[int(level) - 1]
+        t["e" + level] = np.array([2.0 - 2.0 * np.cos(2.0 * np.pi * k / n) for _, k in order])
+    t["c3"] = np.array([np.cos(2.0 * np.pi * k / (m // 4)) for _, k in orders[2]], np.float32)
+    fine = np.eye(2 * m)
+    lap = 2.0 * fine - np.roll(fine, 1, 0) - np.roll(fine, -1, 0)
+    current = interpolation(m, range(2 * m), CUBIC) @ bases[0]
+    for i in range(3):
+        t[f"m{i}"] = np.sum(analysis(bases[0]).T * ((0.5 * pairs(m)) @ current), axis=0)
+        current = lap @ current
+    return t
+
+
+def window_cells(count, reach):
+    return [j if j < count + reach else None for j in range(count)] + [
+        count + j if j < reach else (j - 8 if j >= 8 - reach else None) for j in range(8)
+    ]
+
+
+def synthesis(t, cells, weights):
+    m = t["waves"].shape[0]
+    rows = interpolation(m, [0 if cell is None else cell for cell in cells], weights)
+    rows[[cell is None for cell in cells]] = 0.0
+    return rows @ t["waves"]
+
+
+def halves(matrix, axis):
+    high = np.asarray(matrix, jnp.bfloat16)
+    low = np.asarray(matrix - high.astype(np.float64), jnp.bfloat16)
+    return np.concatenate([high, low], axis=axis)
+
+
+def fast_constants(block, sizes):
+    b0, b1, b2 = block
+    m0, m1, m2 = (size // 2 for size in sizes)
+    t0, t1, t2 = (factors(m) for m in (m0, m1, m2))
+    index = np.arange(m0 * m1).reshape(2, 2, m0 // 4, 2, 2, m1 // 4).transpose(0, 3, 1, 4, 2, 5).reshape(-1)
+    i0, i1 = index // m1, index % m1
+    rows2 = m0 * m1 // 4
+    j0, j1 = i0[:rows2], i1[:rows2]
+
+    def across(name, k, l, op=np.multiply):
+        return op(t0[name][k], t1[name][l])
+
+    def joint(a, c):
+        return t0[a][i0] * t1[c][i1]
+
+    columns = [across("r1", i0, i1), across("p1", i0, i1), across("q1", i0, i1), across("e1", i0, i1, np.add)]
+    columns += [joint("m0", "m0"), joint("m1", "m0") + joint("m0", "m1")]
+    columns += [joint("m2", "m0") + joint("m0", "m2") + 2.0 * joint("m1", "m1")]
+    by_row = np.zeros((m0 * m1, 128))
+    by_row[:, : len(columns)] = np.stack(columns, axis=1)
+    for n, name in enumerate(("r2", "p2", "q2", "e2")):
+        by_row[:rows2, 8 + n] = across(name, j0, j1, np.add if name == "e2" else np.multiply)
+    by_lane = np.zeros((16, m2))
+    for n, name in enumerate(("r1", "p1", "q1", "e1", "m0", "m1", "m2")):
+        by_lane[n] = t2[name]
+    for n, name in enumerate(("r2", "p2", "q2", "e2")):
+        by_lane[8 + n, : m2 // 2] = t2[name]
+    two = np.float32(2.0)
+    eigen = np.float32(6.0) - two * t0["c3"][:, None, None]
+    eigen = eigen - two * t1["c3"][None, :, None] - two * t2["c3"][None, None, :]
+    eigen = (np.float32(0.25 ** (LEVELS - 1)) * eigen).reshape(rows2 // 4, m2 // 4)
+    table = {"by_row": by_row, "by_lane": by_lane, "eigen": np.concatenate([eigen, eigen], axis=1)}
+    table = {name: np.asarray(value, np.float32) for name, value in table.items()}
+
+    half = b2 // 2
+    own = np.zeros((2, b2, 3, 2, half))
+    four = sum(np.roll(np.kron(np.eye(half), np.eye(2)[:, :1]), s, axis=0) for s in (-1, 0, 1, 2))
+    four[b2 - 1, 0] = 0.0
+    four[0, half - 1] = 0.0
+    beside = np.zeros((b2, half))
+    beside[b2 - 1, 0] = beside[0, half - 1] = 1.0
+    for n, part in enumerate((pairs(half).T, beside, four)):
+        for s in range(2):
+            own[s, :, n, s] = 0.125 * part
+    table = {"own": np.asarray(own.reshape(2 * b2, 3 * b2), jnp.bfloat16), **table}
+
+    forward = analysis(t0["waves"])[i0][:, :, None] * analysis(t1["waves"])[i1][:, None, :]
+    table["forward_rows"] = halves(forward.reshape(m0 * m1, m0 * m1), 1)
+    table["forward_lanes"] = halves(analysis(t2["waves"]).T, 0)
+    lane_cells = [j if j < b2 + b2 // 2 else j - 2 * b2 for j in range(2 * b2)]
+    for name, weights, reach in (("cubic", CUBIC, 2), ("linear", LINEAR, 1)):
+        planes = synthesis(t0, range(-reach, b0 + reach), weights)[:, i0]
+        rows = synthesis(t1, window_cells(b1, reach), weights)[:, i1]
+        full = planes[:, None, :] * rows[None, :, :]
+        table[name + "_rows"] = halves(full.reshape(-1, m0 * m1), 1)
+        table[name + "_lanes"] = halves(synthesis(t2, lane_cells, weights).T, 0)
+    return table
+
+
+def split(values):
+    high = values.astype(jnp.bfloat16)
+    return high, (values - high.astype(jnp.float32)).astype(jnp.bfloat16)
+
+
+def by_right(values, table):
+    high, low = split(values)
+    depth = values.shape[1]
+    first, second = table[:depth], table[depth:]
+    return jnp.dot(
+        jnp.concatenate([high, low, high], axis=1),
+        jnp.concatenate([first, first, second], axis=0),
+        preferred_element_type=jnp.float32,
+    )
+
+
+def by_left(table, values):
+    high, low = split(values)
+    depth = values.shape[0]
+    first, second = table[:, :depth], table[:, depth:]
+    return jnp.dot(
+        jnp.concatenate([first, first, second], axis=1),
+        jnp.concatenate([high, low, high], axis=0),
+        preferred_element_type=jnp.float32,
+    )
+
+
+def fold(values):
+    rows = values.shape[0] // 4
+    total = (values[:rows] + values[rows : 2 * rows]) + (values[2 * rows : 3 * rows] + values[3 * rows :])
+    return total + pltpu.roll(total, total.shape[1] // 2, 1)
+
+
+def unfold(values):
+    return jnp.concatenate([values] * 4, axis=0)
+
+
+def own_parts(source, own, outs, alpha, beta):
+    block, across, along_rows, along_planes, rest = outs
+    b0, b1, b2 = source.shape
+    h0, h1 = b0 // 2, b1 // 2
+    first = [source[p, pl.ds(0, h1, stride=2), :] for p in range(b0)]
+    second = [source[p, pl.ds(1, h1, stride=2), :] for p in range(b0)]
+    summed = [a + b for a, b in zip(first, second)]
+    row = lax.broadcasted_iota(jnp.int32, (h1, b2), 0)
+    zero = jnp.zeros((h1, b2), jnp.float32)
+    whole, faces, inner = [], [], []
+    for c in range(h0):
+        total = summed[2 * c] + summed[2 * c + 1]
+        down = pltpu.roll(second[2 * c] + second[2 * c + 1], 1, 0)
+        up = pltpu.roll(first[2 * c] + first[2 * c + 1], h1 - 1, 0)
+        whole.append(total)
+        faces.append(jnp.where(row == 0, down, jnp.where(row == h1 - 1, up, zero)))
+        near = 2.0 * total + jnp.where(row > 0, down, zero) + jnp.where(row < h1 - 1, up, zero)
+        if c > 0:
+            near = near + summed[2 * c - 1]
+        if c < h0 - 1:
+            near = near + summed[2 * c + 2]
+        inner.append(near)
+
+    def pack(planes):
+        half = len(planes) // 2
+        return [jnp.concatenate([planes[i], planes[i + half]], axis=1) for i in range(half)]
+
+    ends = [jnp.concatenate([summed[b0 - 1], summed[0]], axis=1)]
+    stacked = jnp.concatenate(pack(whole) + pack(faces) + pack(inner) + ends + [jnp.zeros((8, 2 * b2), jnp.float32)], axis=0)
+    parts = parts_of(stacked, 3)
+    weights = own[...]
+    result = jnp.dot(
+        jnp.concatenate(parts, axis=1),
+        jnp.concatenate([weights] * 3, axis=0),
+        preferred_element_type=jnp.float32,
+    )
+    n = h0 // 2 * h1
+    shape = block.shape
+    mine = result[:n, :b2]
+    block[...] = mine.reshape(shape)
+    across[...] = result[:n, b2 : 2 * b2].reshape(shape)
+    along_rows[...] = result[n : 2 * n, :b2].reshape(shape)
+    along_planes[...] = result[3 * n : 3 * n + h1, :b2]
+    rest[...] = (alpha * mine + beta * (result[2 * n : 3 * n, :b2] + result[:n, 2 * b2 :])).reshape(shape)
+
+
+def beyond(place, counts):
+    x, y, z = place
+    return (x, lax.rem(y - 1 + 2 * lax.rem(y, 2) + counts[1], counts[1]), z)
+
+
+def send_all(counts, block, landing, sems):
+    send, recv, relay_send, relay_recv = sems
+    me = position()
+    mine = landing.at[slot(me, counts)]
+    copies = []
+    for n, offset in enumerate(chip_offsets(counts)):
+        copies.append(remote(block, mine, send.at[n], recv.at[n], shifted(me, counts, offset)))
+        copies[-1].start()
+    n = len(copies)
+    relays = [remote(block, mine, relay_send.at[n], relay_recv.at[n], partner_of(me))]
+    relays[-1].start()
+    return copies, relays
+
+
+def relay_all(counts, started, landing, sems):
+    relay_send, relay_recv = sems[2:]
+    me = position()
+    copies, relays = started
+    for n, offset in enumerate(chip_offsets(counts)):
+        copies[n].wait_recv()
+        source = shifted(me, counts, tuple(-step for step in offset))
+        arrived = landing.at[slot(source, counts)]
+        relays.append(remote(arrived, arrived, relay_send.at[n], relay_recv.at[n], partner_of(me)))
+        relays[-1].start()
+
+
+def end_all(counts, started, block, landing):
+    copies, relays = started
+    landing[slot(position(), counts)] = block[...]
+    for copy in copies:
+        copy.wait_send()
+    for copy in relays:
+        copy.wait()
+
+
+def prepare(k, many, few, shift):
+    diagonal0, diagonal1, diagonal2 = (6.0 * 0.25**level + shift for level in range(3))
+    sigma0, sigma1, sigma2 = diagonal0 - 6.0, diagonal1 - 1.5, diagonal2 - 0.375
+    damp0, damp1, damp2 = DAMPING / diagonal0, DAMPING / diagonal1, DAMPING / diagonal2
+    down, pre, fine_q, out_q, out_g, out_e, cross = many
+    by_row, by_lane = k["by_row"], k["by_lane"]
+    lanes = by_lane.shape[1]
+
+    def level1(i):
+        rows = pl.ds(pl.multiple_of(8 * i, 8), 8)
+        column = by_row[rows, :]
+
+        def tall(n):
+            return jnp.broadcast_to(column[:, n : n + 1], (8, lanes))
+
+        def wide(n):
+            return jnp.broadcast_to(by_lane[n : n + 1, :], (8, lanes))
+
+        r, p, q = (tall(n) * wide(n) for n in range(3))
+        a = 0.25 * (tall(3) + wide(3)) + sigma1
+        s = 1.0 - damp1 * a
+        down[rows, :] = r
+        pre[rows, :] = r * s
+        fine_q[rows, :] = a * q
+        out_q[rows, :] = s * s * q
+        out_g[rows, :] = damp1 * (1.0 + s)
+        out_e[rows, :] = s * p
+        c0, c1, c2 = tall(4), tall(5), tall(6)
+        first = sigma0 * c0 + c1 - damp0 * ((sigma0 * sigma0) * c0 + (2.0 * sigma0) * c1 + c2)
+        second = c0 - (2.0 * damp0) * (sigma0 * c0 + c1)
+        cross[rows, :] = first * wide(4) + second * wide(5) - (damp0 * c0) * wide(6)
+
+    loop(by_row.shape[0] // 8, level1)
+    rows2, lanes2 = few[0].shape
+    column = by_row[:rows2, :]
+
+    def tall(n):
+        return jnp.broadcast_to(column[:, n : n + 1], (rows2, lanes2))
+
+    def wide(n):
+        return jnp.broadcast_to(by_lane[n : n + 1, :lanes2], (rows2, lanes2))
+
+    r, p, q = (tall(n) * wide(n) for n in (8, 9, 10))
+    a = 0.0625 * (tall(11) + wide(11)) + sigma2
+    s = 1.0 - damp2 * a
+    values = (r, r * s, a * q, s * s * q, damp2 * (1.0 + s), s * p)
+    for ref, value in zip(few, values):
+        ref[...] = value
+    k["inverse"][...] = 1.0 / (k["eigen"][...] + shift)
+
+
+def level2(k, few, g):
+    down, pre, fine_q, out_q, out_g, out_e = few
+    e = unfold(fold(pre[...] * g) * k["inverse"][...])
+    return out_g[...] * g + out_e[...] * e
+
+
+def level2_full(k, few, g):
+    down, pre, fine_q, out_q, out_g, out_e = few
+    start = unfold(fold(down[...] * g) * k["inverse"][...])
+    e = unfold(fold(pre[...] * (g - fine_q[...] * start)) * k["inverse"][...])
+    return out_q[...] * start + out_g[...] * g + out_e[...] * e
+
+
+def blocks_of(spectrum, i):
+    rows2, lanes2 = spectrum.shape[0] // 4, spectrum.shape[1] // 2
+    for a in range(4):
+        start = pl.multiple_of(a * rows2 + 8 * i, 8)
+        for c in range(2):
+            yield (pl.ds(start, 8), pl.ds(c * lanes2, lanes2))
+
+
+def spectral_u(k, many, few, spectrum, coupled, coarse):
+    down, pre, fine_q, out_q, out_g, out_e, cross = many
+    first, second, third = coarse
+    steps = first.shape[0] // 8
+
+    def at(i):
+        return pl.ds(pl.multiple_of(8 * i, 8), 8)
+
+    def restrict(i):
+        first[at(i), :] = sum(down[w] * spectrum[w] for w in blocks_of(spectrum, i))
+
+    loop(steps, restrict)
+    second[...] = level2_full(k, few, first[...])
+
+    def residue(i):
+        u = second[at(i), :]
+        first[at(i), :] = sum(pre[w] * (spectrum[w] - fine_q[w] * u) for w in blocks_of(spectrum, i))
+
+    loop(steps, residue)
+    third[...] = level2(k, few, first[...])
+
+    def finish(i):
+        u, e = second[at(i), :], third[at(i), :]
+        for w in blocks_of(spectrum, i):
+            value = out_q[w] * u + out_g[w] * spectrum[w] + out_e[w] * e
+            spectrum[w] = value
+            coupled[w] = cross[w] * value
+
+    loop(steps, finish)
+
+
+def spectral_e(k, many, few, spectrum, coupled, coarse):
+    pre, out_g, out_e = many[1], many[4], many[5]
+    first, second = coarse[:2]
+    steps = first.shape[0] // 8
+
+    def at(i):
+        return pl.ds(pl.multiple_of(8 * i, 8), 8)
+
+    def residue(i):
+        total = None
+        for w in blocks_of(spectrum, i):
+            value = spectrum[w] - coupled[w]
+            spectrum[w] = value
+            total = pre[w] * value if total is None else total + pre[w] * value
+        first[at(i), :] = total
+
+    loop(steps, residue)
+    second[...] = level2(k, few, first[...])
+
+    def finish(i):
+        e = second[at(i), :]
+        for w in blocks_of(spectrum, i):
+            spectrum[w] = out_g[w] * spectrum[w] + out_e[w] * e
+
+    loop(steps, finish)
+
+
+def transform(k, counts, landing, g, spectrum):
+    unpack(landing, counts, g)
+    m0, m1, m2 = g.shape
+    spectrum[...] = by_left(k["forward_rows"], by_right(g[...].reshape(m0 * m1, m2), k["forward_lanes"]))
+
+
+def evaluate(k, kind, spectrum, out):
+    values = by_right(by_left(k[kind + "_rows"], spectrum[...]), k[kind + "_lanes"])
+    out[...] = values.reshape(out.shape)
+
+
+def neighbours_of(v, p):
+    center = v[p]
+    return center, v[p - 1] + v[p + 1] + around(center)
+
+
+def fast_kernel(names, counts, *refs):
+    count = len(names)
+    outside = dict(zip(names, refs))
+    shift_ref, source_ref, out, *rest = refs[count:]
+    k = dict(zip(names, rest[:count]))
+    rest = rest[count:]
+    landing_f, landing_h = rest[:2]
+    faces_in = rest[2:8]
+    halos = rest[8:11]
+    block_f, block_h, across, along_rows, along_planes, local = rest[11:17]
+    own_planes, own_rows, own_columns = rest[17:20]
+    many, few, coarse = rest[20:27], rest[27:33], rest[33:36]
+    k["inverse"], g, spectrum, coupled, wide, w, f, source = rest[36:44]
+    table_sems, face_send, face_recv, halo_send, halo_recv = rest[44:49]
+    sems_f, sems_h = rest[49:53], rest[53:57]
+
+    shift = shift_ref[0]
+    me = position()
+    barrier = pltpu.get_barrier_semaphore()
+    places = [shifted(me, counts, offset) for offset in chip_offsets(counts)]
+    places += [partner_of(me), beyond(me, counts)]
+    greet(barrier, places)
+    loads = {"source": pltpu.make_async_copy(source_ref, source, table_sems.at[count])}
+    loads["source"].start()
+    for n, name in enumerate(names):
+        loads[name] = pltpu.make_async_copy(outside[name], k[name], table_sems.at[n])
+        loads[name].start()
+
+    b0, b1, b2 = source.shape
+    diagonal = 6.0 + shift
+    damp = DAMPING / diagonal
+    loads["source"].wait()
+    loads["own"].wait()
+    parts = (block_f, across, along_rows, along_planes, local)
+    own_parts(source, k["own"], parts, 1.0 - damp * diagonal, damp)
+    own_planes[0] = source[0]
+    own_planes[1] = source[b0 - 1]
+    own_rows[0] = source[:, pl.ds(0, 1), :]
+    own_rows[1] = source[:, pl.ds(b1 - 1, 1), :]
+    turned = source[...].reshape(b0 * b1, b2).T
+    own_columns[0] = turned[:8]
+    own_columns[1] = turned[b2 - 8 :]
+    pl.semaphore_wait(barrier, len(places))
+
+    faces = face_offsets(counts)
+    order = (0, 2, 1)
+    sent = (along_planes, along_rows, across)
+    first = []
+    for n, (offset, axis, side) in enumerate(faces):
+        place = shifted(me, counts, offset)
+        copy = remote(sent[order[axis]], faces_in[2 * order[axis] + 1 - side], face_send.at[n], face_recv.at[n], place)
+        copy.start()
+        first.append(copy)
+    started_f = send_all(counts, block_f, landing_f, sems_f)
+    buffers = ((own_planes, halos[0]), (own_rows, halos[1]), (own_columns, halos[2]))
+    last = []
+    for n, (offset, axis, side) in enumerate(faces):
+        mine, halo = buffers[order[axis]]
+        place = shifted(me, counts, offset)
+        last.append(remote(mine.at[side], halo.at[1 - side], halo_send.at[n], halo_recv.at[n], place))
+        last[-1].start()
+
+    for name in ("by_row", "by_lane", "eigen"):
+        loads[name].wait()
+    prepare(k, many, few, shift)
+    for copy in first:
+        copy.wait()
+    shape = local.shape
+    lane = lax.rem(lax.broadcasted_iota(jnp.int32, shape, 2), b2 // 2)
+    row = lax.broadcasted_iota(jnp.int32, shape, 1)
+    from_planes, from_rows, from_lanes = faces_in[:2], faces_in[2:4], faces_in[4:6]
+    total = jnp.where(lane == 0, from_lanes[0][...], 0.0) + jnp.where(lane == b2 // 2 - 1, from_lanes[1][...], 0.0)
+    total = total + jnp.where(row == 0, from_rows[0][...], 0.0) + jnp.where(row == shape[1] - 1, from_rows[1][...], 0.0)
+    block_h[...] = local[...] + damp * total
+    low = lax.broadcasted_iota(jnp.int32, shape[1:], 1) < b2 // 2
+    block_h[0] = block_h[0] + damp * jnp.where(low, from_planes[0][...], 0.0)
+    end = shape[0] - 1
+    block_h[end] = block_h[end] + damp * jnp.where(low, 0.0, from_planes[1][...])
+    started_h = send_all(counts, block_h, landing_h, sems_h)
+
+    relay_all(counts, started_f, landing_f, sems_f)
+    for copy in last:
+        copy.wait()
+    f[...] = jnp.zeros_like(f)
+    rows, lanes = pl.ds(0, b1), pl.ds(0, b2)
+    f[1 : b0 + 1, rows, lanes] = source[...]
+    f[0, rows, lanes] = halos[0][0]
+    f[b0 + 1, rows, lanes] = halos[0][1]
+    f[1 : b0 + 1, pl.ds(b1, 1), lanes] = halos[1][1]
+    f[1 : b0 + 1, pl.ds(b1 + 7, 1), lanes] = halos[1][0]
+    middle = jnp.zeros((b2 - 16, b0 * b1), jnp.float32)
+    turned = jnp.concatenate([halos[2][1], middle, halos[2][0]], axis=0)
+    f[1 : b0 + 1, rows, pl.ds(b2, b2)] = turned.T.reshape(b0, b1, b2)
+    end_all(counts, started_f, block_f, landing_f)
+    for name in names:
+        if name not in ("own", "by_row", "by_lane", "eigen"):
+            loads[name].wait()
+    transform(k, counts, landing_f, g, spectrum)
+    spectral_u(k, many, few, spectrum, coupled, coarse)
+
+    relay_all(counts, started_h, landing_h, sems_h)
+    evaluate(k, "cubic", spectrum, wide)
+    keep = 1.0 - damp * diagonal
+
+    def before(p):
+        center, beside = neighbours_of(wide, p + 1)
+        f[p] = keep * center + damp * (beside + f[p])
+
+    loop(b0 + 2, before)
+    end_all(counts, started_h, block_h, landing_h)
+    transform(k, counts, landing_h, g, spectrum)
+    spectral_e(k, many, few, spectrum, coupled, coarse)
+    evaluate(k, "linear", spectrum, w)
+
+    def add(p):
+        w[p] = w[p] + f[p]
+
+    loop(b0 + 2, add)
+
+    def after(p):
+        center, beside = neighbours_of(w, p + 1)
+        out[p] = (keep * center + damp * beside)[:b1, :b2] + damp * source[p]
+
+    loop(b0, after)
+
+
+def fast_per_device(counts, source, shift):
+    nx, ny, nz = counts
+    b0, b1, b2 = source.shape
+    sizes = (b0 * nx, b1 * nz, b2 * ny)
+    table = fast_constants(source.shape, sizes)
+    m0, m1, m2 = (size // 2 for size in sizes)
+    rows = m0 * m1
+    packed = (b0 // 4, b1 // 2, b2)
+    devices = nx * ny * nz
+    chips = devices // 2
+    vmem = pl.BlockSpec(memory_space=pltpu.VMEM)
+
+    def field(*shape):
+        return pltpu.VMEM(shape, jnp.float32)
+
+    def in_hbm(value):
+        return pltpu.with_memory_space_constraint(value, pltpu.HBM)
+
+    names = tuple(table)
+    scratch = [pltpu.VMEM(table[name].shape, table[name].dtype) for name in names]
+    scratch += [field(devices, *packed)] * 2
+    scratch += [field(*packed[1:])] * 2 + [field(*packed)] * 4
+    scratch += [field(2, b1, b2), field(2, b0, 1, b2), field(2, 8, b0 * b1)]
+    scratch += [field(*packed)] * 4 + [field(*packed[1:]), field(*packed)]
+    scratch += [field(2, b1, b2), field(2, b0, 1, b2), field(2, 8, b0 * b1)]
+    scratch += [field(rows, m2)] * 7 + [field(rows // 4, m2 // 2)] * 9
+    scratch += [field(rows // 16, m2 // 2), field(m0, m1, m2), field(rows, m2), field(rows, m2)]
+    scratch += [field(b0 + 4, b1 + 8, 2 * b2), field(b0 + 2, b1 + 8, 2 * b2), field(b0 + 2, b1 + 8, 2 * b2)]
+    scratch += [field(*source.shape)]
+    dma = pltpu.SemaphoreType.DMA
+    scratch += [dma((len(names) + 1,))] + [dma((6,))] * 4
+    scratch += ([dma((max(chips - 1, 1),))] * 2 + [dma((chips,))] * 2) * 2
+    return pl.pallas_call(
+        functools.partial(fast_kernel, names, counts),
+        out_shape=jax.ShapeDtypeStruct(source.shape, jnp.float32),
+        in_specs=[pl.BlockSpec(memory_space=pltpu.HBM)] * len(names)
+        + [pl.BlockSpec(memory_space=pltpu.SMEM), pl.BlockSpec(memory_space=pltpu.HBM)],
+        out_specs=vmem,
+        scratch_shapes=scratch,
+        compiler_params=pltpu.CompilerParams(
+            vmem_limit_bytes=40 * 1024 * 1024, collective_id=0, has_side_effects=True
+        ),
+    )(*[in_hbm(jnp.asarray(table[name])) for name in names], shift, in_hbm(source))
+
+
+def small_enough(counts, block):
+    (nx, ny, nz), (b0, b1, b2) = counts, block
+    rows = (b0 * nx // 2) * (b1 * nz // 2)
+    return rows <= 512 and rows % 128 == 0 and b2 == 128 and b1 == 16 and b0 % 4 == 0 and ny * b2 % 512 == 0 and min(counts) > 1
+
+
+def dispatch(counts, source, shift):
+    run = fast_per_device if small_enough(counts, source.shape) else per_device
+    return run(counts, source, shift)
+
+
 def solution(mesh):
     counts = tuple(mesh.shape[name] for name in NAMES)
     return jax.shard_map(
-        functools.partial(per_device, counts),
+        functools.partial(dispatch, counts),
         mesh=mesh,
         in_specs=(P("gx", "gz", "gy"), P()),
         out_specs=P("gx", "gz", "gy"),

time: 42.9 us -> 28.2 us (0.66)
  Pallas kernels: 40.5 us -> 26.7 us
  local copies, waits for them, and re-layouts: 1.57 us -> 0.66 us
    pallas_call x1, Pallas kernels: 40.5 us -> 26.7 us  [fast_per_device(): pl.pallas_call(functools.partial(fast_kernel, names, counts), out_shape=j...]
    unnamed x1, local copies, waits for them, and re-layouts: 1.57 us -> 0.66 us
where the time goes in v1:
time: 28.2 us; the launch traced here: 28 us
  Pallas kernels  26.7 us (95%)
  local copies, waits for them, and re-layouts  0.66 us (2%)
  between operations  0.66 us (2%)
    pallas_call x1, Pallas kernels, fast_per_device(): pl.pallas_call(functools.partial(fast_kernel, names, counts), out_shape=j...  26.7 us
    unnamed x1, local copies, waits for them, and re-layouts  0.66 us

profile of v1, /device:TPU:0, one launch (start us, length us, event | category | flops | bytes accessed | tf_op | source)
XLA Modules:
  0.0 28.0 jit_solution(11385447196463458434)
XLA Ops:
  0.7 26.7 %shard_map.118 = f32[16,16,128]{2,1,0:T(8,128)S(1)} custom-call(bf16[256,384]{1,0:T(8,128)(2,1)} %constant.20.clone.refs_0_, f32[512,128]{1,0:T(8,128)} %constant.21.clone.refs_1_, f32[16,256]{1,0:T(8,128)} %constant.22.clone.refs_2_, f32[32,128]{1,0:T(8,128)} %constant.23.clone.refs_3_, bf16[512,1024]{1,0:T(8,128)(2,1)} %constant.24.clone.refs_4_, ...), custom_call_target="tpu_custom_call" | custom-call | tf_op jit(solution)/shard_map/pallas_call | solution.py:1151
  27.4 0.7 %copy.15 = f32[16,16,128]{2,1,0:T(8,128)} copy(f32[16,16,128]{2,1,0:T(8,128)S(1)} %shard_map.118) | data formatting | bytes 262144

commit v2 on v1

--- a/solution.py
+++ b/solution.py
@@ -643,17 +643,42 @@
     return t
 
 
-def window_cells(count, reach):
-    return [j if j < count + reach else None for j in range(count)] + [
-        count + j if j < reach else (j - 8 if j >= 8 - reach else None) for j in range(8)
+def near(matrix, axis=0):
+    return np.roll(matrix, 1, axis) + np.roll(matrix, -1, axis)
+
+
+def synthesis(t, cells, weights, powers):
+    m = t["waves"].shape[0]
+    matrix = interpolation(m, range(2 * m), weights) @ t["waves"]
+    result = []
+    for _ in range(powers):
+        result.append(matrix[np.array(cells) % (2 * m)])
+        matrix = near(matrix)
+    return result
+
+
+def pick(matrix, rows, columns):
+    return matrix[np.array(rows) % matrix.shape[0]][:, np.array(columns) % matrix.shape[1]]
+
+
+def late_kinds(m, rows, columns):
+    plain = interpolation(m, range(2 * m), LINEAR)
+    return [pick(kind, rows, columns) for kind in (plain, near(plain), near(plain, 1), near(near(plain), 1))]
+
+
+def mixed(p, r):
+    return [
+        np.kron(p[0], r[0]),
+        np.kron(p[1], r[0]) + np.kron(p[0], r[1]),
+        np.kron(p[2], r[0]) + np.kron(p[0], r[2]),
+        np.kron(p[3], r[0]) + np.kron(p[0], r[3]) + np.kron(p[2], r[1]) + np.kron(p[1], r[2]),
     ]
 
 
-def synthesis(t, cells, weights):
-    m = t["waves"].shape[0]
-    rows = interpolation(m, [0 if cell is None else cell for cell in cells], weights)
-    rows[[cell is None for cell in cells]] = 0.0
-    return rows @ t["waves"]
+def exact(matrix):
+    result = np.asarray(matrix, jnp.bfloat16)
+    assert np.all(result.astype(np.float64) == matrix)
+    return result
 
 
 def halves(matrix, axis):
@@ -662,14 +687,58 @@
     return np.concatenate([high, low], axis=axis)
 
 
-def fast_constants(block, sizes):
+def halved_rows(m0, m1):
+    index = np.arange(m0 * m1).reshape(2, 2, 2, m0 // 8, 2, 2, m1 // 4)
+    index = index.transpose(2, 0, 4, 1, 5, 3, 6).reshape(2, 4, -1)
+    return index, index[:, 0].reshape(-1), index.reshape(-1)
+
+
+def own_table(half):
+    count = 2 * half
+    four = sum(np.roll(np.kron(np.eye(half), np.eye(2)[:, :1]), s, axis=0) for s in (-1, 0, 1, 2))
+    four[count - 1, 0] = 0.0
+    four[0, half - 1] = 0.0
+    beside = np.zeros((count, half))
+    beside[count - 1, 0] = beside[0, half - 1] = 1.0
+    own = np.zeros((2, count, 3, 2, half))
+    for n, part in enumerate((pairs(half).T, beside, four)):
+        for s in range(2):
+            own[s, :, n, s] = 0.125 * part
+    return np.asarray(own.reshape(2 * count, 3 * count), jnp.bfloat16)
+
+
+def two_levels(count):
+    whole = 2 * count
+    fine, half = np.eye(whole), np.eye(whole // 2)
+    near, near1 = (np.roll(e, 1, 0) + np.roll(e, -1, 0) for e in (fine, half))
+    down, down1 = pairs(whole // 2), pairs(whole // 4)
+    start = count // 2
+    rows = range(start // 4 - 1, (start + count) // 4 + 1)
+    kinds = (down1 @ down, down1 @ down @ near, down1 @ near1 @ down, down1 @ near1 @ down @ near)
+    return [kind[rows, start : start + count] for kind in kinds]
+
+
+def early_tables(block):
+    b0, b1, b2 = block
+    (p, r, c) = ([*two_levels(size)] for size in block)
+    full = mixed(p, r)
+    rows = np.zeros((4, 3, 16, b0 * b1))
+    rows[:, :, : 2 * r[0].shape[0]] = np.stack(full).reshape(4, 3, 2 * r[0].shape[0], b0 * b1)
+    lanes = np.zeros((4, b2, b2))
+    for n in range(4):
+        lanes[n, :, : c[n].shape[0]] = c[n].T / 64.0
+    return exact(rows.reshape(-1, b0 * b1)), exact(lanes.reshape(-1, b2))
+
+
+def fast_constants(counts, block, sizes):
+    nx, ny, nz = counts
     b0, b1, b2 = block
     m0, m1, m2 = (size // 2 for size in sizes)
     t0, t1, t2 = (factors(m) for m in (m0, m1, m2))
-    index = np.arange(m0 * m1).reshape(2, 2, m0 // 4, 2, 2, m1 // 4).transpose(0, 3, 1, 4, 2, 5).reshape(-1)
-    i0, i1 = index // m1, index % m1
-    rows2 = m0 * m1 // 4
-    j0, j1 = i0[:rows2], i1[:rows2]
+    parts, index2, index1 = halved_rows(m0, m1)
+    i0, i1 = index1 // m1, index1 % m1
+    j0, j1 = index2 // m1, index2 % m1
+    rows2 = len(index2)
 
     def across(name, k, l, op=np.multiply):
         return op(t0[name][k], t1[name][l])
@@ -693,31 +762,48 @@
     eigen = np.float32(6.0) - two * t0["c3"][:, None, None]
     eigen = eigen - two * t1["c3"][None, :, None] - two * t2["c3"][None, None, :]
     eigen = (np.float32(0.25 ** (LEVELS - 1)) * eigen).reshape(rows2 // 4, m2 // 4)
-    table = {"by_row": by_row, "by_lane": by_lane, "eigen": np.concatenate([eigen, eigen], axis=1)}
-    table = {name: np.asarray(value, np.float32) for name, value in table.items()}
-
-    half = b2 // 2
-    own = np.zeros((2, b2, 3, 2, half))
-    four = sum(np.roll(np.kron(np.eye(half), np.eye(2)[:, :1]), s, axis=0) for s in (-1, 0, 1, 2))
-    four[b2 - 1, 0] = 0.0
-    four[0, half - 1] = 0.0
-    beside = np.zeros((b2, half))
-    beside[b2 - 1, 0] = beside[0, half - 1] = 1.0
-    for n, part in enumerate((pairs(half).T, beside, four)):
-        for s in range(2):
-            own[s, :, n, s] = 0.125 * part
-    table = {"own": np.asarray(own.reshape(2 * b2, 3 * b2), jnp.bfloat16), **table}
-
-    forward = analysis(t0["waves"])[i0][:, :, None] * analysis(t1["waves"])[i1][:, None, :]
-    table["forward_rows"] = halves(forward.reshape(m0 * m1, m0 * m1), 1)
+    early_rows, early_lanes = early_tables(block)
+    table = {"own": own_table(b2 // 2), "early_rows": early_rows, "early_lanes": early_lanes}
+    small = {"by_row": by_row, "by_lane": by_lane, "eigen": np.concatenate([eigen, eigen], axis=1)}
+    table.update({name: np.asarray(value, np.float32) for name, value in small.items()})
+
+    a0, a1 = (analysis(waves(m // 2, modes(m // 2, 1))) for m in (m0, m1))
+    a2 = analysis(waves(m2 // 2, modes(m2 // 2, 1)))
+    p0, p1, p2 = b0 // 4, b1 // 4, b2 // 4
+    wide = p2 + 2
+    lanes = np.zeros((ny, b2, 3, m2 // 2))
+    for dy in range(ny):
+        for n in range(3):
+            lanes[dy, 42 * n : 42 * n + wide, n] = a2[:, np.arange(p2 * dy - 1, p2 * dy + p2 + 1) % (m2 // 2)].T
+    table["level2_lanes"] = halves(lanes.reshape(ny * b2, -1), 0)
+    n, dx, dz, c, r = np.meshgrid(*(range(k) for k in (3, nx, nz, 2, p1 + 2)), indexing="ij")
+    planes = (p0 * dx + 2 * n + c - 1 - p0 // 2) % (m0 // 2)
+    rows = (p1 * dz + r - 1) % (m1 // 2)
+    full = np.zeros((rows2, 3, nx, nz, 16))
+    full[..., : 2 * (p1 + 2)] = (a0[j0][:, planes] * a1[j1][:, rows]).reshape(rows2, 3, nx, nz, -1)
+    table["level2_rows"] = halves(full.reshape(rows2, -1), 1)
+
+    forward = analysis(t0["waves"])[i0][:, : m0 // 2, None] * analysis(t1["waves"])[i1][:, None, :]
+    table["forward_rows"] = halves(forward.reshape(2, m0 * m1 // 2, -1), 2)
     table["forward_lanes"] = halves(analysis(t2["waves"]).T, 0)
-    lane_cells = [j if j < b2 + b2 // 2 else j - 2 * b2 for j in range(2 * b2)]
-    for name, weights, reach in (("cubic", CUBIC, 2), ("linear", LINEAR, 1)):
-        planes = synthesis(t0, range(-reach, b0 + reach), weights)[:, i0]
-        rows = synthesis(t1, window_cells(b1, reach), weights)[:, i1]
-        full = planes[:, None, :] * rows[None, :, :]
-        table[name + "_rows"] = halves(full.reshape(-1, m0 * m1), 1)
-        table[name + "_lanes"] = halves(synthesis(t2, lane_cells, weights).T, 0)
+    for name, weights, powers in (("cubic", CUBIC, 3), ("linear", LINEAR, 2)):
+        p = synthesis(t0, range(b0 // 2), weights, powers)
+        r = synthesis(t1, range(b1), weights, powers)
+        full = []
+        for part in parts.reshape(2, -1):
+            q0 = [matrix[:, part // m1][:, None, :] for matrix in p]
+            q1 = [matrix[:, part % m1][None, :, :] for matrix in r]
+            kinds = [q0[0] * q1[0], q0[1] * q1[0] + q0[0] * q1[1]]
+            if powers == 3:
+                kinds.append(q0[2] * q1[0] + 2.0 * q0[1] * q1[1] + q0[0] * q1[2])
+            full.append(np.stack(kinds).reshape(-1, part.size))
+        table[name + "_rows"] = halves(np.stack(full), 2)
+        lanes = [matrix.T for matrix in synthesis(t2, range(b2), weights, powers)]
+        table[name + "_lanes"] = halves(np.concatenate(lanes), 0)
+    p = late_kinds(m0, range(b0), range(-2, b0 // 2 + 2))
+    r = late_kinds(m1, range(b1), range(m1))
+    table["late_rows"] = exact(np.concatenate(mixed(p, r), axis=1))
+    table["late_lanes"] = exact(np.concatenate([c.T for c in late_kinds(m2, range(b2), range(m2))], axis=1))
     return table
 
 
@@ -749,13 +835,18 @@
 
 
 def fold(values):
-    rows = values.shape[0] // 4
-    total = (values[:rows] + values[rows : 2 * rows]) + (values[2 * rows : 3 * rows] + values[3 * rows :])
+    n = values.shape[0] // 8
+    parts = []
+    for kind in range(2):
+        quarter = [values[(4 * kind + i) * n : (4 * kind + i + 1) * n] for i in range(4)]
+        parts.append((quarter[0] + quarter[1]) + (quarter[2] + quarter[3]))
+    total = jnp.concatenate(parts, axis=0)
     return total + pltpu.roll(total, total.shape[1] // 2, 1)
 
 
 def unfold(values):
-    return jnp.concatenate([values] * 4, axis=0)
+    n = values.shape[0] // 2
+    return jnp.concatenate([values[:n]] * 4 + [values[n:]] * 4, axis=0)
 
 
 def own_parts(source, own, outs, alpha, beta):
@@ -804,18 +895,66 @@
     rest[...] = (alpha * mine + beta * (result[2 * n : 3 * n, :b2] + result[:n, 2 * b2 :])).reshape(shape)
 
 
+def early_part(source, rows_table, lanes_table, weights):
+    keep0, near0, keep1, near1 = weights
+    b0, b1, b2 = source.shape
+    result = jnp.dot(
+        jnp.concatenate([rows_table[...]] * 3, axis=1),
+        jnp.concatenate(parts_of(source[...].reshape(b0 * b1, b2), 3), axis=0),
+        preferred_element_type=jnp.float32,
+    )
+    n = result.shape[0] // 4
+    plain, first, second, both = (result[i * n : (i + 1) * n] for i in range(4))
+    joint = near0 * near1
+    columns = (
+        (keep0 * keep1) * plain + (keep1 * near0) * first + (keep0 * near1) * second + joint * both,
+        (keep1 * near0) * plain + joint * second,
+        (keep0 * near1) * plain + joint * first,
+        joint * plain,
+    )
+    result = jnp.dot(
+        jnp.concatenate(parts_of(jnp.concatenate(columns, axis=1), 3), axis=1),
+        jnp.concatenate([lanes_table[...]] * 3, axis=0),
+        preferred_element_type=jnp.float32,
+    )
+    total = result[:16] + pltpu.roll(result[16:32], 42, 1)
+    return (total + pltpu.roll(result[32:], 84, 1)).reshape(2, 8, b2)
+
+
 def beyond(place, counts):
     x, y, z = place
     return (x, lax.rem(y - 1 + 2 * lax.rem(y, 2) + counts[1], counts[1]), z)
 
 
-def send_all(counts, block, landing, sems):
+def close_by(counts):
+    chosen = []
+    for offset in chip_offsets(counts):
+        step = offset[0]
+        if min(step, counts[0] - step) <= 1:
+            part = 0 if step == 0 or counts[0] == 2 else (1 if step == 1 else -1)
+            chosen.append((offset, part))
+    return chosen
+
+
+def everywhere(counts):
+    return [(offset, 0) for offset in chip_offsets(counts)]
+
+
+def piece(ref, part):
+    if part == 0:
+        return ref
+    half = ref.shape[0] // 2
+    return ref.at[pl.ds(half if part == 1 else 0, half)]
+
+
+def send_all(counts, chosen, block, landing, sems):
     send, recv, relay_send, relay_recv = sems
     me = position()
     mine = landing.at[slot(me, counts)]
     copies = []
-    for n, offset in enumerate(chip_offsets(counts)):
-        copies.append(remote(block, mine, send.at[n], recv.at[n], shifted(me, counts, offset)))
+    for n, (offset, part) in enumerate(chosen):
+        place = shifted(me, counts, offset)
+        copies.append(remote(piece(block, part), piece(mine, part), send.at[n], recv.at[n], place))
         copies[-1].start()
     n = len(copies)
     relays = [remote(block, mine, relay_send.at[n], relay_recv.at[n], partner_of(me))]
@@ -823,14 +962,14 @@
     return copies, relays
 
 
-def relay_all(counts, started, landing, sems):
+def relay_all(counts, chosen, started, landing, sems):
     relay_send, relay_recv = sems[2:]
     me = position()
     copies, relays = started
-    for n, offset in enumerate(chip_offsets(counts)):
+    for n, (offset, part) in enumerate(chosen):
         copies[n].wait_recv()
         source = shifted(me, counts, tuple(-step for step in offset))
-        arrived = landing.at[slot(source, counts)]
+        arrived = piece(landing.at[slot(source, counts)], part)
         relays.append(remote(arrived, arrived, relay_send.at[n], relay_recv.at[n], partner_of(me)))
         relays[-1].start()
 
@@ -842,6 +981,19 @@
         copy.wait_send()
     for copy in relays:
         copy.wait()
+
+
+def exchange(counts, sent, received, send, recv):
+    me = position()
+    order = (0, 2, 1)
+    copies = []
+    for n, (offset, axis, side) in enumerate(face_offsets(counts)):
+        which = order[axis]
+        mine = sent[which] if len(sent[which]) == 1 else [sent[which][side]]
+        place = shifted(me, counts, offset)
+        copies.append(remote(mine[0], received[2 * which + 1 - side], send.at[n], recv.at[n], place))
+        copies[-1].start()
+    return copies
 
 
 def prepare(k, many, few, shift):
@@ -910,8 +1062,10 @@
 
 def blocks_of(spectrum, i):
     rows2, lanes2 = spectrum.shape[0] // 4, spectrum.shape[1] // 2
+    half = rows2 // 2
+    base = 8 * i + 3 * half * lax.div(i, half // 8)
     for a in range(4):
-        start = pl.multiple_of(a * rows2 + 8 * i, 8)
+        start = pl.multiple_of(base + a * half, 8)
         for c in range(2):
             yield (pl.ds(start, 8), pl.ds(c * lanes2, lanes2))
 
@@ -939,72 +1093,174 @@
 
     def finish(i):
         u, e = second[at(i), :], third[at(i), :]
+        total = None
         for w in blocks_of(spectrum, i):
             value = out_q[w] * u + out_g[w] * spectrum[w] + out_e[w] * e
             spectrum[w] = value
-            coupled[w] = cross[w] * value
-
-    loop(steps, finish)
-
-
-def spectral_e(k, many, few, spectrum, coupled, coarse):
-    pre, out_g, out_e = many[1], many[4], many[5]
-    first, second = coarse[:2]
-    steps = first.shape[0] // 8
-
-    def at(i):
-        return pl.ds(pl.multiple_of(8 * i, 8), 8)
-
-    def residue(i):
-        total = None
-        for w in blocks_of(spectrum, i):
-            value = spectrum[w] - coupled[w]
-            spectrum[w] = value
+            value = cross[w] * value
+            coupled[w] = value
             total = pre[w] * value if total is None else total + pre[w] * value
         first[at(i), :] = total
 
-    loop(steps, residue)
-    second[...] = level2(k, few, first[...])
+    loop(steps, finish)
+
+
+def spectral_e(many, spectrum, coupled, e2):
+    out_g, out_e = many[4], many[5]
 
     def finish(i):
-        e = second[at(i), :]
+        e = e2[pl.ds(pl.multiple_of(8 * i, 8), 8), :]
         for w in blocks_of(spectrum, i):
-            spectrum[w] = out_g[w] * spectrum[w] + out_e[w] * e
-
-    loop(steps, finish)
+            spectrum[w] = out_e[w] * e - out_g[w] * coupled[w]
+
+    loop(e2.shape[0] // 8, finish)
+
+
+def unpack_centred(gathered, counts, g):
+    nx, ny, nz = counts
+    me = position()
+    half, rows, lanes = gathered.shape[1:]
+    planes = g.shape[0]
+    low = lax.broadcasted_iota(jnp.int32, (half, rows, lanes), 2) < lanes // 2
+    for dx in range(nx):
+        for dz in range(nz):
+            for pair in range(ny // 2):
+                parts = [
+                    gathered[slot(shifted(me, counts, (dx, dy, dz)), counts)] for dy in (2 * pair, 2 * pair + 1)
+                ]
+                turned = [pltpu.roll(part, lanes // 2, 2) for part in parts]
+                where = (pl.ds(dz * rows, rows), pl.ds(pair * lanes, lanes))
+                start = (2 * half * dx - half) % planes
+                g[(pl.ds(start, half), *where)] = jnp.where(low, parts[0], turned[1])
+                g[(pl.ds(2 * half * dx, half), *where)] = jnp.where(low, turned[0], parts[1])
 
 
 def transform(k, counts, landing, g, spectrum):
-    unpack(landing, counts, g)
+    unpack_centred(landing, counts, g)
     m0, m1, m2 = g.shape
-    spectrum[...] = by_left(k["forward_rows"], by_right(g[...].reshape(m0 * m1, m2), k["forward_lanes"]))
-
-
-def evaluate(k, kind, spectrum, out):
-    values = by_right(by_left(k[kind + "_rows"], spectrum[...]), k[kind + "_lanes"])
-    out[...] = values.reshape(out.shape)
-
-
-def neighbours_of(v, p):
-    center = v[p]
-    return center, v[p - 1] + v[p + 1] + around(center)
+    half = m0 // 2
+    depth = half * m1
+    for kind in range(2):
+        rows = [g[p] - g[m0 - 1 - p] if kind else g[p] + g[m0 - 1 - p] for p in range(half)]
+        values = by_left(k["forward_rows"][kind], jnp.concatenate(rows, axis=0))
+        spectrum[kind * depth : (kind + 1) * depth, :] = by_right(values, k["forward_lanes"])
+
+
+def transform2(k, counts, landing):
+    nx, ny, nz = counts
+    me = position()
+    columns = []
+    for dy in range(ny):
+        rows = [
+            landing[slot(shifted(me, counts, (dx, dy, dz)), counts)].reshape(16, -1)
+            for dx in range(nx)
+            for dz in range(nz)
+        ]
+        columns.append(jnp.concatenate(rows, axis=0))
+    values = by_right(jnp.concatenate(columns, axis=1), k["level2_lanes"])
+    width = values.shape[1] // 3
+    parts = [values[:, n * width : (n + 1) * width] for n in range(3)]
+    return by_left(k["level2_rows"], jnp.concatenate(parts, axis=0))
+
+
+def evaluate(k, kind, spectrum, mix, out):
+    planes, rows, lanes = out.shape
+    half = planes // 2
+    depth = spectrum.shape[0] // 2
+    parts = []
+    for n in range(2):
+        values = by_left(k[kind + "_rows"][n], spectrum[n * depth : (n + 1) * depth, :])
+        pieces = [values[i : i + half * rows] for i in range(0, values.shape[0], half * rows)]
+        columns = [sum(c * pieces[i] for i, c in enumerate(line) if c is not None) for line in mix]
+        parts.append(by_right(jnp.concatenate(columns, axis=1), k[kind + "_lanes"]).reshape(half, rows, lanes))
+    even, odd = parts
+    for p in range(half):
+        for index, value in ((half + p, even[p] + odd[p]), (half - 1 - p, even[p] - odd[p])):
+            out[index] = out[index] + value
+
+
+def unpack_near(gathered, counts, g):
+    nx, ny, nz = counts
+    me = position()
+    half, rows, lanes = gathered.shape[1:]
+    for dx, first, last in ((nx - 1, half - 2, half), (0, 0, half), (1, 0, 2)):
+        shape = (last - first, rows, lanes)
+        low = lax.broadcasted_iota(jnp.int32, shape, 2) < lanes // 2
+        for dz in range(nz):
+            for pair in range(ny // 2):
+                parts = [
+                    gathered[slot(shifted(me, counts, (dx, dy, dz)), counts), pl.ds(first, last - first)]
+                    for dy in (2 * pair, 2 * pair + 1)
+                ]
+                turned = [pltpu.roll(part, lanes // 2, 2) for part in parts]
+                where = (pl.ds(dz * rows, rows), pl.ds(pair * lanes, lanes))
+                if dx != nx - 1:
+                    start = 2 if dx == 0 else 2 + 2 * half
+                    g[(pl.ds(start, last - first), *where)] = jnp.where(low, parts[0], turned[1])
+                if dx != 1:
+                    start = 2 + half if dx == 0 else 0
+                    g[(pl.ds(start, last - first), *where)] = jnp.where(low, turned[0], parts[1])
+
+
+def late_part(k, g, weights):
+    keep0, near0, keep1, near1 = weights
+    planes, m1, m2 = g.shape
+    pieces = split(g[...].reshape(planes * m1, m2))
+    table = k["late_lanes"][...]
+    values = jnp.dot(
+        jnp.concatenate(pieces, axis=1),
+        jnp.concatenate([table, table], axis=0),
+        preferred_element_type=jnp.float32,
+    )
+    lanes = values.shape[1] // 4
+    a, b, c, d = (values[:, i * lanes : (i + 1) * lanes] for i in range(4))
+    joint = near0 * near1
+    stacked = (
+        (keep0 * keep1) * a + (near0 * keep1) * b + (keep0 * near1) * c + joint * d,
+        (near0 * keep1) * a + joint * c,
+        (keep0 * near1) * a + joint * b,
+        joint * a,
+    )
+    table = k["late_rows"][...]
+    values = jnp.dot(
+        jnp.concatenate([table, table], axis=1),
+        jnp.concatenate(split(jnp.concatenate(stacked, axis=0)), axis=0),
+        preferred_element_type=jnp.float32,
+    )
+    return values
+
+
+def own_sweep(f, source, keep, damp, out):
+    rows, lanes = source.shape[1:]
+
+    def body(p):
+        beside = f[p] + f[p + 2] + around(f[p + 1])
+        out[p] = damp * ((1.0 + keep) * source[p] + damp * beside[:rows, :lanes])
+
+    loop(source.shape[0], body)
 
 
 def fast_kernel(names, counts, *refs):
     count = len(names)
     outside = dict(zip(names, refs))
     shift_ref, source_ref, out, *rest = refs[count:]
-    k = dict(zip(names, rest[:count]))
-    rest = rest[count:]
-    landing_f, landing_h = rest[:2]
-    faces_in = rest[2:8]
-    halos = rest[8:11]
-    block_f, block_h, across, along_rows, along_planes, local = rest[11:17]
-    own_planes, own_rows, own_columns = rest[17:20]
-    many, few, coarse = rest[20:27], rest[27:33], rest[33:36]
-    k["inverse"], g, spectrum, coupled, wide, w, f, source = rest[36:44]
-    table_sems, face_send, face_recv, halo_send, halo_recv = rest[44:49]
-    sems_f, sems_h = rest[49:53], rest[53:57]
+
+    def take(number):
+        taken = rest[:number]
+        del rest[:number]
+        return taken
+
+    k = dict(zip(names, take(count)))
+    (source,) = take(1)
+    landing_f, landing_h, landing_j = take(3)
+    faces_in, halos = take(6), take(3)
+    block_f, block_h, across, along_rows, local, along_planes = take(6)
+    (block_j,) = take(1)
+    own_planes, own_rows, own_columns = take(3)
+    many, few, coarse = take(7), take(6), take(3)
+    k["inverse"], g, near_h, spectrum, coupled, f = take(6)
+    table_sems, *face_sems = take(5)
+    sems_f, sems_h, sems_j = take(4), take(4), take(4)
 
     shift = shift_ref[0]
     me = position()
@@ -1019,8 +1275,8 @@
         loads[name].start()
 
     b0, b1, b2 = source.shape
-    diagonal = 6.0 + shift
-    damp = DAMPING / diagonal
+    diagonal, diagonal1 = 6.0 + shift, 1.5 + shift
+    damp, damp1 = DAMPING / diagonal, DAMPING / diagonal1
     loads["source"].wait()
     loads["own"].wait()
     parts = (block_f, across, along_rows, along_planes, local)
@@ -1032,25 +1288,15 @@
     turned = source[...].reshape(b0 * b1, b2).T
     own_columns[0] = turned[:8]
     own_columns[1] = turned[b2 - 8 :]
+    for name in ("early_rows", "early_lanes"):
+        loads[name].wait()
+    weights = (1.0 - damp * diagonal, damp, 1.0 - damp1 * diagonal1, 0.25 * damp1)
+    block_j[...] = early_part(source, k["early_rows"], k["early_lanes"], weights)
     pl.semaphore_wait(barrier, len(places))
 
-    faces = face_offsets(counts)
-    order = (0, 2, 1)
-    sent = (along_planes, along_rows, across)
-    first = []
-    for n, (offset, axis, side) in enumerate(faces):
-        place = shifted(me, counts, offset)
-        copy = remote(sent[order[axis]], faces_in[2 * order[axis] + 1 - side], face_send.at[n], face_recv.at[n], place)
-        copy.start()
-        first.append(copy)
-    started_f = send_all(counts, block_f, landing_f, sems_f)
-    buffers = ((own_planes, halos[0]), (own_rows, halos[1]), (own_columns, halos[2]))
-    last = []
-    for n, (offset, axis, side) in enumerate(faces):
-        mine, halo = buffers[order[axis]]
-        place = shifted(me, counts, offset)
-        last.append(remote(mine.at[side], halo.at[1 - side], halo_send.at[n], halo_recv.at[n], place))
-        last[-1].start()
+    first = exchange(counts, ([along_planes], [along_rows], [across]), faces_in, *face_sems[:2])
+    started_f = send_all(counts, everywhere(counts), block_f, landing_f, sems_f)
+    started_j = send_all(counts, everywhere(counts), block_j, landing_j, sems_j)
 
     for name in ("by_row", "by_lane", "eigen"):
         loads[name].wait()
@@ -1068,9 +1314,11 @@
     block_h[0] = block_h[0] + damp * jnp.where(low, from_planes[0][...], 0.0)
     end = shape[0] - 1
     block_h[end] = block_h[end] + damp * jnp.where(low, 0.0, from_planes[1][...])
-    started_h = send_all(counts, block_h, landing_h, sems_h)
-
-    relay_all(counts, started_f, landing_f, sems_f)
+
+    mine = [[own.at[side] for side in range(2)] for own in (own_planes, own_rows, own_columns)]
+    last = exchange(counts, mine, [halo.at[side] for halo in halos for side in range(2)], *face_sems[2:4])
+    started_h = send_all(counts, close_by(counts), block_h, landing_h, sems_h)
+    relay_all(counts, everywhere(counts), started_f, landing_f, sems_f)
     for copy in last:
         copy.wait()
     f[...] = jnp.zeros_like(f)
@@ -1083,50 +1331,40 @@
     middle = jnp.zeros((b2 - 16, b0 * b1), jnp.float32)
     turned = jnp.concatenate([halos[2][1], middle, halos[2][0]], axis=0)
     f[1 : b0 + 1, rows, pl.ds(b2, b2)] = turned.T.reshape(b0, b1, b2)
+    keep = 1.0 - damp * diagonal
+    own_sweep(f, source, keep, damp, out)
     end_all(counts, started_f, block_f, landing_f)
     for name in names:
-        if name not in ("own", "by_row", "by_lane", "eigen"):
+        if name not in ("own", "early_rows", "early_lanes", "by_row", "by_lane", "eigen"):
             loads[name].wait()
     transform(k, counts, landing_f, g, spectrum)
     spectral_u(k, many, few, spectrum, coupled, coarse)
-
-    relay_all(counts, started_h, landing_h, sems_h)
-    evaluate(k, "cubic", spectrum, wide)
-    keep = 1.0 - damp * diagonal
-
-    def before(p):
-        center, beside = neighbours_of(wide, p + 1)
-        f[p] = keep * center + damp * (beside + f[p])
-
-    loop(b0 + 2, before)
+    relay_all(counts, everywhere(counts), started_j, landing_j, sems_j)
+    relay_all(counts, close_by(counts), started_h, landing_h, sems_h)
+    double = 2.0 * keep * damp
+    square = damp * damp
+    mix = ((keep * keep, double, square), (double, 2.0 * square, None), (square, None, None))
+    evaluate(k, "cubic", spectrum, mix, out)
     end_all(counts, started_h, block_h, landing_h)
-    transform(k, counts, landing_h, g, spectrum)
-    spectral_e(k, many, few, spectrum, coupled, coarse)
-    evaluate(k, "linear", spectrum, w)
-
-    def add(p):
-        w[p] = w[p] + f[p]
-
-    loop(b0 + 2, add)
-
-    def after(p):
-        center, beside = neighbours_of(w, p + 1)
-        out[p] = (keep * center + damp * beside)[:b1, :b2] + damp * source[p]
-
-    loop(b0, after)
+    end_all(counts, started_j, block_j, landing_j)
+    unpack_near(landing_h, counts, near_h)
+    keep1 = 1.0 - damp1 * diagonal1
+    coarse[1][...] = level2(k, few, transform2(k, counts, landing_j) - coarse[0][...])
+    late = late_part(k, near_h, (keep, damp, damp1 * (1.0 + keep1), 0.25 * damp1 * damp1))
+    out[...] = out[...] + late.reshape(out.shape)
+    spectral_e(many, spectrum, coupled, coarse[1])
+    evaluate(k, "linear", spectrum, ((keep, damp), (damp, None)), out)
 
 
 def fast_per_device(counts, source, shift):
     nx, ny, nz = counts
     b0, b1, b2 = source.shape
     sizes = (b0 * nx, b1 * nz, b2 * ny)
-    table = fast_constants(source.shape, sizes)
+    table = fast_constants(counts, source.shape, sizes)
     m0, m1, m2 = (size // 2 for size in sizes)
     rows = m0 * m1
     packed = (b0 // 4, b1 // 2, b2)
     devices = nx * ny * nz
-    chips = devices // 2
-    vmem = pl.BlockSpec(memory_space=pltpu.VMEM)
 
     def field(*shape):
         return pltpu.VMEM(shape, jnp.float32)
@@ -1135,25 +1373,25 @@
         return pltpu.with_memory_space_constraint(value, pltpu.HBM)
 
     names = tuple(table)
+    tile = packed[1:]
+    fine = [field(2, b1, b2), field(2, b0, 1, b2), field(2, 8, b0 * b1)]
     scratch = [pltpu.VMEM(table[name].shape, table[name].dtype) for name in names]
-    scratch += [field(devices, *packed)] * 2
-    scratch += [field(*packed[1:])] * 2 + [field(*packed)] * 4
-    scratch += [field(2, b1, b2), field(2, b0, 1, b2), field(2, 8, b0 * b1)]
-    scratch += [field(*packed)] * 4 + [field(*packed[1:]), field(*packed)]
-    scratch += [field(2, b1, b2), field(2, b0, 1, b2), field(2, 8, b0 * b1)]
+    scratch += [field(*source.shape), field(devices, *packed), field(devices, *packed), field(devices, 2, *tile)]
+    scratch += [field(*tile)] * 2 + [field(*packed)] * 4 + fine
+    scratch += [field(*packed)] * 5 + [field(*tile), field(2, *tile)] + fine
     scratch += [field(rows, m2)] * 7 + [field(rows // 4, m2 // 2)] * 9
-    scratch += [field(rows // 16, m2 // 2), field(m0, m1, m2), field(rows, m2), field(rows, m2)]
-    scratch += [field(b0 + 4, b1 + 8, 2 * b2), field(b0 + 2, b1 + 8, 2 * b2), field(b0 + 2, b1 + 8, 2 * b2)]
-    scratch += [field(*source.shape)]
+    scratch += [field(rows // 16, m2 // 2), field(m0, m1, m2), field(b0 // 2 + 4, m1, m2)]
+    scratch += [field(rows, m2), field(rows, m2), field(b0 + 2, b1 + 8, 2 * b2)]
     dma = pltpu.SemaphoreType.DMA
     scratch += [dma((len(names) + 1,))] + [dma((6,))] * 4
-    scratch += ([dma((max(chips - 1, 1),))] * 2 + [dma((chips,))] * 2) * 2
+    for chosen in (everywhere(counts), close_by(counts), everywhere(counts)):
+        scratch += [dma((len(chosen),))] * 2 + [dma((len(chosen) + 1,))] * 2
     return pl.pallas_call(
         functools.partial(fast_kernel, names, counts),
         out_shape=jax.ShapeDtypeStruct(source.shape, jnp.float32),
         in_specs=[pl.BlockSpec(memory_space=pltpu.HBM)] * len(names)
         + [pl.BlockSpec(memory_space=pltpu.SMEM), pl.BlockSpec(memory_space=pltpu.HBM)],
-        out_specs=vmem,
+        out_specs=pl.BlockSpec(memory_space=pltpu.VMEM),
         scratch_shapes=scratch,
         compiler_params=pltpu.CompilerParams(
             vmem_limit_bytes=40 * 1024 * 1024, collective_id=0, has_side_effects=True
@@ -1164,7 +1402,7 @@
 def small_enough(counts, block):
     (nx, ny, nz), (b0, b1, b2) = counts, block
     rows = (b0 * nx // 2) * (b1 * nz // 2)
-    return rows <= 512 and rows % 128 == 0 and b2 == 128 and b1 == 16 and b0 % 4 == 0 and ny * b2 % 512 == 0 and min(counts) > 1
+    return rows <= 512 and rows % 128 == 0 and (b0, b1, b2) == (16, 16, 128) and ny % 4 == 0 and min(counts) > 1
 
 
 def dispatch(counts, source, shift):

time: 28.2 us -> 25.3 us (0.90)
  Pallas kernels: 26.7 us -> 23.7 us
    pallas_call x1, Pallas kernels: 26.7 us -> 23.7 us  [fast_per_device(): pl.pallas_call(functools.partial(fast_kernel, names, counts), out_shape=j...]
where the time goes in v2:
time: 25.3 us; the launch traced here: 25.1 us
  Pallas kernels  23.7 us (94%)
  local copies, waits for them, and re-layouts  0.66 us (3%)
  between operations  0.66 us (3%)
    pallas_call x1, Pallas kernels, fast_per_device(): pl.pallas_call(functools.partial(fast_kernel, names, counts), out_shape=j...  23.7 us
    unnamed x1, local copies, waits for them, and re-layouts  0.66 us

profile of v2, /device:TPU:0, one launch (start us, length us, event | category | flops | bytes accessed | tf_op | source)
XLA Modules:
  0.0 25.1 jit_solution(7939638532453162071)
XLA Ops:
  0.7 23.7 %shard_map.172 = f32[16,16,128]{2,1,0:T(8,128)S(1)} custom-call(bf16[256,384]{1,0:T(8,128)(2,1)} %constant.32.clone.refs_0_, bf16[192,256]{1,0:T(8,128)(2,1)} %constant.33.clone.refs_1_, bf16[512,128]{1,0:T(8,128)(2,1)} %constant.34.clone.refs_2_, f32[512,128]{1,0:T(8,128)} %constant.35.clone.refs_3_, f32[16,256]{1,0:T(8,128)} %constant.36.clone.refs_4_, ...), custom_call_target="tpu_custom_call" | custom-call | tf_op jit(solution)/shard_map/pallas_call | solution.py:1389
  24.4 0.7 %copy.21 = f32[16,16,128]{2,1,0:T(8,128)} copy(f32[16,16,128]{2,1,0:T(8,128)S(1)} %shard_map.172) | data formatting | bytes 262144

commit v3 on v2

--- a/solution.py
+++ b/solution.py
@@ -936,8 +936,62 @@
     return chosen
 
 
-def everywhere(counts):
-    return [(offset, 0) for offset in chip_offsets(counts)]
+def wait_for(ref, sem):
+    pltpu.make_async_copy(ref, ref, sem).wait()
+
+
+class TwoStage:
+    def __init__(self, counts, near, far, block, landing, sems):
+        self.counts, self.near, self.far = counts, near, far
+        self.block, self.landing = block, landing
+        self.sent, self.arrived, self.relay_sent, self.relayed = sems
+        self.count = 0
+
+    def at(self, offset):
+        source = shifted(position(), self.counts, tuple(-step for step in offset))
+        return self.landing.at[slot(source, self.counts)]
+
+    def send(self, source, target, step, sem):
+        place = shifted(position(), self.counts, step)
+        remote(source, target, self.sent.at[0], self.arrived.at[sem], place).start()
+        self.count += 1
+
+    def start(self, offsets):
+        for offset in offsets:
+            sem = self.near.index(offset) if offset in self.near else len(self.near)
+            self.send(self.block, self.at((0, 0, 0)), offset, sem)
+
+    def relay(self, source, target):
+        remote(source, target, self.relay_sent.at[0], self.relayed.at[0], partner_of(position())).start()
+
+    def own(self):
+        self.relay(self.block, self.at((0, 0, 0)))
+
+    def forward(self):
+        for n, first in enumerate(self.near):
+            arrived = self.at(first)
+            wait_for(arrived, self.arrived.at[n])
+            for second in self.far:
+                self.send(arrived, arrived, second, len(self.near) + 1 + n)
+            self.relay(arrived, arrived)
+
+    def rest(self):
+        for n, first in enumerate(((0, 0, 0), *self.near)):
+            wait_for(self.landing.at[pl.ds(0, len(self.far))], self.arrived.at[len(self.near) + n])
+            for second in self.far:
+                arrived = self.at(tuple(a + b for a, b in zip(first, second)))
+                self.relay(arrived, arrived)
+
+    def end(self):
+        self.landing[slot(position(), self.counts)] = self.block[...]
+        wait_for(self.landing.at[pl.ds(0, self.count)], self.sent.at[0])
+        for sem in (self.relay_sent, self.relayed):
+            wait_for(self.landing.at[pl.ds(0, self.count + 1)], sem.at[0])
+
+    @staticmethod
+    def semaphores(near):
+        dma = pltpu.SemaphoreType.DMA
+        return [dma((1,)), dma((2 * len(near) + 1,)), dma((1,)), dma((1,))]
 
 
 def piece(ref, part):
@@ -947,53 +1001,48 @@
     return ref.at[pl.ds(half if part == 1 else 0, half)]
 
 
-def send_all(counts, chosen, block, landing, sems):
-    send, recv, relay_send, relay_recv = sems
-    me = position()
-    mine = landing.at[slot(me, counts)]
-    copies = []
-    for n, (offset, part) in enumerate(chosen):
-        place = shifted(me, counts, offset)
-        copies.append(remote(piece(block, part), piece(mine, part), send.at[n], recv.at[n], place))
-        copies[-1].start()
-    n = len(copies)
-    relays = [remote(block, mine, relay_send.at[n], relay_recv.at[n], partner_of(me))]
-    relays[-1].start()
-    return copies, relays
-
-
-def relay_all(counts, chosen, started, landing, sems):
-    relay_send, relay_recv = sems[2:]
-    me = position()
-    copies, relays = started
-    for n, (offset, part) in enumerate(chosen):
-        copies[n].wait_recv()
-        source = shifted(me, counts, tuple(-step for step in offset))
-        arrived = piece(landing.at[slot(source, counts)], part)
-        relays.append(remote(arrived, arrived, relay_send.at[n], relay_recv.at[n], partner_of(me)))
-        relays[-1].start()
-
-
-def end_all(counts, started, block, landing):
-    copies, relays = started
-    landing[slot(position(), counts)] = block[...]
-    for copy in copies:
-        copy.wait_send()
-    for copy in relays:
-        copy.wait()
+class Close:
+    def __init__(self, counts, chosen, block, landing, sems):
+        self.counts, self.chosen = counts, chosen
+        self.block, self.landing = block, landing
+        self.sent, self.arrived, self.relay_sent, self.relayed = (sem.at[0] for sem in sems)
+        self.blocks = sum(2 if part == 0 else 1 for _, part in chosen) // 2
+
+    def at(self, offset):
+        source = shifted(position(), self.counts, tuple(-step for step in offset))
+        return self.landing.at[slot(source, self.counts)]
+
+    def relay(self, source, target):
+        remote(source, target, self.relay_sent, self.relayed, partner_of(position())).start()
+
+    def start(self):
+        mine = self.at((0, 0, 0))
+        for offset, part in self.chosen:
+            place = shifted(position(), self.counts, offset)
+            remote(piece(self.block, part), piece(mine, part), self.sent, self.arrived, place).start()
+        self.relay(self.block, mine)
+
+    def rest(self):
+        wait_for(self.landing.at[pl.ds(0, self.blocks)], self.arrived)
+        for offset, part in self.chosen:
+            arrived = piece(self.at(offset), part)
+            self.relay(arrived, arrived)
+
+    def end(self):
+        self.landing[slot(position(), self.counts)] = self.block[...]
+        wait_for(self.landing.at[pl.ds(0, self.blocks)], self.sent)
+        for sem in (self.relay_sent, self.relayed):
+            wait_for(self.landing.at[pl.ds(0, self.blocks + 1)], sem)
 
 
 def exchange(counts, sent, received, send, recv):
     me = position()
     order = (0, 2, 1)
-    copies = []
-    for n, (offset, axis, side) in enumerate(face_offsets(counts)):
+    for offset, axis, side in face_offsets(counts):
         which = order[axis]
         mine = sent[which] if len(sent[which]) == 1 else [sent[which][side]]
         place = shifted(me, counts, offset)
-        copies.append(remote(mine[0], received[2 * which + 1 - side], send.at[n], recv.at[n], place))
-        copies[-1].start()
-    return copies
+        remote(mine[0], received[2 * which + 1 - side], send.at[0], recv.at[0], place).start()
 
 
 def prepare(k, many, few, shift):
@@ -1294,15 +1343,20 @@
     block_j[...] = early_part(source, k["early_rows"], k["early_lanes"], weights)
     pl.semaphore_wait(barrier, len(places))
 
-    first = exchange(counts, ([along_planes], [along_rows], [across]), faces_in, *face_sems[:2])
-    started_f = send_all(counts, everywhere(counts), block_f, landing_f, sems_f)
-    started_j = send_all(counts, everywhere(counts), block_j, landing_j, sems_j)
+    exchange(counts, ([along_planes], [along_rows], [across]), faces_in, *face_sems[:2])
+    along, across_all = stages(counts)
+    gather_f = TwoStage(counts, along[::-1], across_all, block_f, landing_f, sems_f)
+    gather_j = TwoStage(counts, across_all[::-1], along, block_j, landing_j, sems_j)
+    gather_f.start(along + across_all)
+    gather_j.start(across_all)
+    gather_f.own()
+    gather_j.own()
 
     for name in ("by_row", "by_lane", "eigen"):
         loads[name].wait()
     prepare(k, many, few, shift)
-    for copy in first:
-        copy.wait()
+    for sem in face_sems[:2]:
+        wait_for(f.at[pl.ds(0, 3)], sem.at[0])
     shape = local.shape
     lane = lax.rem(lax.broadcasted_iota(jnp.int32, shape, 2), b2 // 2)
     row = lax.broadcasted_iota(jnp.int32, shape, 1)
@@ -1315,12 +1369,16 @@
     end = shape[0] - 1
     block_h[end] = block_h[end] + damp * jnp.where(low, 0.0, from_planes[1][...])
 
+    gather_f.forward()
     mine = [[own.at[side] for side in range(2)] for own in (own_planes, own_rows, own_columns)]
-    last = exchange(counts, mine, [halo.at[side] for halo in halos for side in range(2)], *face_sems[2:4])
-    started_h = send_all(counts, close_by(counts), block_h, landing_h, sems_h)
-    relay_all(counts, everywhere(counts), started_f, landing_f, sems_f)
-    for copy in last:
-        copy.wait()
+    exchange(counts, mine, [halo.at[side] for halo in halos for side in range(2)], *face_sems[2:4])
+    gather_j.start(along)
+    gather_j.forward()
+    close_h = Close(counts, close_by(counts), block_h, landing_h, sems_h)
+    close_h.start()
+    gather_f.rest()
+    for sem in face_sems[2:4]:
+        wait_for(f.at[pl.ds(0, 2)], sem.at[0])
     f[...] = jnp.zeros_like(f)
     rows, lanes = pl.ds(0, b1), pl.ds(0, b2)
     f[1 : b0 + 1, rows, lanes] = source[...]
@@ -1333,20 +1391,20 @@
     f[1 : b0 + 1, rows, pl.ds(b2, b2)] = turned.T.reshape(b0, b1, b2)
     keep = 1.0 - damp * diagonal
     own_sweep(f, source, keep, damp, out)
-    end_all(counts, started_f, block_f, landing_f)
+    gather_f.end()
     for name in names:
         if name not in ("own", "early_rows", "early_lanes", "by_row", "by_lane", "eigen"):
             loads[name].wait()
     transform(k, counts, landing_f, g, spectrum)
     spectral_u(k, many, few, spectrum, coupled, coarse)
-    relay_all(counts, everywhere(counts), started_j, landing_j, sems_j)
-    relay_all(counts, close_by(counts), started_h, landing_h, sems_h)
+    gather_j.rest()
+    close_h.rest()
     double = 2.0 * keep * damp
     square = damp * damp
     mix = ((keep * keep, double, square), (double, 2.0 * square, None), (square, None, None))
     evaluate(k, "cubic", spectrum, mix, out)
-    end_all(counts, started_h, block_h, landing_h)
-    end_all(counts, started_j, block_j, landing_j)
+    close_h.end()
+    gather_j.end()
     unpack_near(landing_h, counts, near_h)
     keep1 = 1.0 - damp1 * diagonal1
     coarse[1][...] = level2(k, few, transform2(k, counts, landing_j) - coarse[0][...])
@@ -1383,9 +1441,9 @@
     scratch += [field(rows // 16, m2 // 2), field(m0, m1, m2), field(b0 // 2 + 4, m1, m2)]
     scratch += [field(rows, m2), field(rows, m2), field(b0 + 2, b1 + 8, 2 * b2)]
     dma = pltpu.SemaphoreType.DMA
-    scratch += [dma((len(names) + 1,))] + [dma((6,))] * 4
-    for chosen in (everywhere(counts), close_by(counts), everywhere(counts)):
-        scratch += [dma((len(chosen),))] * 2 + [dma((len(chosen) + 1,))] * 2
+    scratch += [dma((len(names) + 1,))] + [dma((1,))] * 4
+    along, across = stages(counts)
+    scratch += TwoStage.semaphores(along) + [dma((1,))] * 4 + TwoStage.semaphores(across)
     return pl.pallas_call(
         functools.partial(fast_kernel, names, counts),
         out_shape=jax.ShapeDtypeStruct(source.shape, jnp.float32),

time: 25.3 us -> 22.9 us (0.905)
  Pallas kernels: 23.7 us -> 21.5 us
    pallas_call x1, Pallas kernels: 23.7 us -> 21.5 us  [fast_per_device(): pl.pallas_call(functools.partial(fast_kernel, names, counts), out_shape=j...]
where the time goes in v3:
time: 22.9 us; the launch traced here: 22.8 us
  Pallas kernels  21.5 us (94%)
  local copies, waits for them, and re-layouts  0.66 us (3%)
  between operations  0.66 us (3%)
    pallas_call x1, Pallas kernels, fast_per_device(): pl.pallas_call(functools.partial(fast_kernel, names, counts), out_shape=j...  21.5 us
    unnamed x1, local copies, waits for them, and re-layouts  0.66 us

profile of v3, /device:TPU:0, one launch (start us, length us, event | category | flops | bytes accessed | tf_op | source)
XLA Modules:
  0.0 22.8 jit_solution(5874472802759585321)
XLA Ops:
  0.7 21.5 %shard_map.172 = f32[16,16,128]{2,1,0:T(8,128)S(1)} custom-call(bf16[256,384]{1,0:T(8,128)(2,1)} %constant.32.clone.refs_0_, bf16[192,256]{1,0:T(8,128)(2,1)} %constant.33.clone.refs_1_, bf16[512,128]{1,0:T(8,128)(2,1)} %constant.34.clone.refs_2_, f32[512,128]{1,0:T(8,128)} %constant.35.clone.refs_3_, f32[16,256]{1,0:T(8,128)} %constant.36.clone.refs_4_, ...), custom_call_target="tpu_custom_call" | custom-call | tf_op jit(solution)/shard_map/pallas_call | solution.py:1447
  22.1 0.7 %copy.21 = f32[16,16,128]{2,1,0:T(8,128)} copy(f32[16,16,128]{2,1,0:T(8,128)S(1)} %shard_map.172) | data formatting | bytes 262144

commit v4 on v3

--- a/solution.py
+++ b/solution.py
@@ -926,16 +926,6 @@
     return (x, lax.rem(y - 1 + 2 * lax.rem(y, 2) + counts[1], counts[1]), z)
 
 
-def close_by(counts):
-    chosen = []
-    for offset in chip_offsets(counts):
-        step = offset[0]
-        if min(step, counts[0] - step) <= 1:
-            part = 0 if step == 0 or counts[0] == 2 else (1 if step == 1 else -1)
-            chosen.append((offset, part))
-    return chosen
-
-
 def wait_for(ref, sem):
     pltpu.make_async_copy(ref, ref, sem).wait()
 
@@ -967,9 +957,9 @@
     def own(self):
         self.relay(self.block, self.at((0, 0, 0)))
 
-    def forward(self):
-        for n, first in enumerate(self.near):
-            arrived = self.at(first)
+    def forward(self, which):
+        for n in which:
+            arrived = self.at(self.near[n])
             wait_for(arrived, self.arrived.at[n])
             for second in self.far:
                 self.send(arrived, arrived, second, len(self.near) + 1 + n)
@@ -1002,37 +992,51 @@
 
 
 class Close:
-    def __init__(self, counts, chosen, block, landing, sems):
-        self.counts, self.chosen = counts, chosen
-        self.block, self.landing = block, landing
-        self.sent, self.arrived, self.relay_sent, self.relayed = (sem.at[0] for sem in sems)
-        self.blocks = sum(2 if part == 0 else 1 for _, part in chosen) // 2
+    def __init__(self, counts, near, block, landing, sems):
+        self.counts, self.near, self.block, self.landing = counts, near, block, landing
+        self.far = [((1, 0, 0), 1), ((counts[0] - 1, 0, 0), -1)] if counts[0] > 2 else [((1, 0, 0), 0)]
+        self.sent, self.arrived, self.relay_sent, self.relayed = sems
+        self.blocks = 2 * len(near) + 1
 
     def at(self, offset):
         source = shifted(position(), self.counts, tuple(-step for step in offset))
         return self.landing.at[slot(source, self.counts)]
 
+    def send(self, source, target, step, sem):
+        place = shifted(position(), self.counts, step)
+        remote(source, target, self.sent.at[0], self.arrived.at[sem], place).start()
+
     def relay(self, source, target):
-        remote(source, target, self.relay_sent, self.relayed, partner_of(position())).start()
+        remote(source, target, self.relay_sent.at[0], self.relayed.at[0], partner_of(position())).start()
 
     def start(self):
         mine = self.at((0, 0, 0))
-        for offset, part in self.chosen:
-            place = shifted(position(), self.counts, offset)
-            remote(piece(self.block, part), piece(mine, part), self.sent, self.arrived, place).start()
+        for n, offset in enumerate(self.near):
+            self.send(self.block, mine, offset, n)
+        for step, part in self.far:
+            self.send(piece(self.block, part), piece(mine, part), step, len(self.near))
         self.relay(self.block, mine)
 
+    def forward(self):
+        for n, first in enumerate(self.near):
+            arrived = self.at(first)
+            wait_for(arrived, self.arrived.at[n])
+            for step, part in self.far:
+                self.send(piece(arrived, part), piece(arrived, part), step, len(self.near) + 1 + n)
+            self.relay(arrived, arrived)
+
     def rest(self):
-        wait_for(self.landing.at[pl.ds(0, self.blocks)], self.arrived)
-        for offset, part in self.chosen:
-            arrived = piece(self.at(offset), part)
-            self.relay(arrived, arrived)
+        for n, first in enumerate(((0, 0, 0), *self.near)):
+            wait_for(self.landing.at[0], self.arrived.at[len(self.near) + n])
+            for step, part in self.far:
+                arrived = piece(self.at(tuple(a + b for a, b in zip(first, step))), part)
+                self.relay(arrived, arrived)
 
     def end(self):
         self.landing[slot(position(), self.counts)] = self.block[...]
-        wait_for(self.landing.at[pl.ds(0, self.blocks)], self.sent)
+        wait_for(self.landing.at[pl.ds(0, self.blocks)], self.sent.at[0])
         for sem in (self.relay_sent, self.relayed):
-            wait_for(self.landing.at[pl.ds(0, self.blocks + 1)], sem)
+            wait_for(self.landing.at[pl.ds(0, self.blocks + 1)], sem.at[0])
 
 
 def exchange(counts, sent, received, send, recv):
@@ -1314,7 +1318,8 @@
     shift = shift_ref[0]
     me = position()
     barrier = pltpu.get_barrier_semaphore()
-    places = [shifted(me, counts, offset) for offset in chip_offsets(counts)]
+    along, across_all = stages(counts)
+    places = [shifted(me, counts, offset) for offset in along + across_all]
     places += [partner_of(me), beyond(me, counts)]
     greet(barrier, places)
     loads = {"source": pltpu.make_async_copy(source_ref, source, table_sems.at[count])}
@@ -1330,6 +1335,13 @@
     loads["own"].wait()
     parts = (block_f, across, along_rows, along_planes, local)
     own_parts(source, k["own"], parts, 1.0 - damp * diagonal, damp)
+    pl.semaphore_wait(barrier, len(places))
+
+    exchange(counts, ([along_planes], [along_rows], [across]), faces_in, *face_sems[:2])
+    gather_f = TwoStage(counts, along[::-1], across_all, block_f, landing_f, sems_f)
+    gather_j = TwoStage(counts, across_all[::-1], along, block_j, landing_j, sems_j)
+    gather_f.start(along + across_all)
+    gather_f.own()
     own_planes[0] = source[0]
     own_planes[1] = source[b0 - 1]
     own_rows[0] = source[:, pl.ds(0, 1), :]
@@ -1341,20 +1353,13 @@
         loads[name].wait()
     weights = (1.0 - damp * diagonal, damp, 1.0 - damp1 * diagonal1, 0.25 * damp1)
     block_j[...] = early_part(source, k["early_rows"], k["early_lanes"], weights)
-    pl.semaphore_wait(barrier, len(places))
-
-    exchange(counts, ([along_planes], [along_rows], [across]), faces_in, *face_sems[:2])
-    along, across_all = stages(counts)
-    gather_f = TwoStage(counts, along[::-1], across_all, block_f, landing_f, sems_f)
-    gather_j = TwoStage(counts, across_all[::-1], along, block_j, landing_j, sems_j)
-    gather_f.start(along + across_all)
     gather_j.start(across_all)
-    gather_f.own()
     gather_j.own()
 
     for name in ("by_row", "by_lane", "eigen"):
         loads[name].wait()
     prepare(k, many, few, shift)
+    gather_f.forward(range(min(2, len(along))))
     for sem in face_sems[:2]:
         wait_for(f.at[pl.ds(0, 3)], sem.at[0])
     shape = local.shape
@@ -1369,14 +1374,15 @@
     end = shape[0] - 1
     block_h[end] = block_h[end] + damp * jnp.where(low, 0.0, from_planes[1][...])
 
-    gather_f.forward()
+    gather_f.forward(range(2, len(along)))
     mine = [[own.at[side] for side in range(2)] for own in (own_planes, own_rows, own_columns)]
     exchange(counts, mine, [halo.at[side] for halo in halos for side in range(2)], *face_sems[2:4])
     gather_j.start(along)
-    gather_j.forward()
-    close_h = Close(counts, close_by(counts), block_h, landing_h, sems_h)
+    gather_j.forward(range(len(across_all)))
+    close_h = Close(counts, across_all[::-1], block_h, landing_h, sems_h)
     close_h.start()
     gather_f.rest()
+    close_h.forward()
     for sem in face_sems[2:4]:
         wait_for(f.at[pl.ds(0, 2)], sem.at[0])
     f[...] = jnp.zeros_like(f)
@@ -1398,20 +1404,20 @@
     transform(k, counts, landing_f, g, spectrum)
     spectral_u(k, many, few, spectrum, coupled, coarse)
     gather_j.rest()
-    close_h.rest()
     double = 2.0 * keep * damp
     square = damp * damp
     mix = ((keep * keep, double, square), (double, 2.0 * square, None), (square, None, None))
     evaluate(k, "cubic", spectrum, mix, out)
+    gather_j.end()
+    coarse[1][...] = level2(k, few, transform2(k, counts, landing_j) - coarse[0][...])
+    close_h.rest()
+    spectral_e(many, spectrum, coupled, coarse[1])
+    evaluate(k, "linear", spectrum, ((keep, damp), (damp, None)), out)
     close_h.end()
-    gather_j.end()
     unpack_near(landing_h, counts, near_h)
     keep1 = 1.0 - damp1 * diagonal1
-    coarse[1][...] = level2(k, few, transform2(k, counts, landing_j) - coarse[0][...])
     late = late_part(k, near_h, (keep, damp, damp1 * (1.0 + keep1), 0.25 * damp1 * damp1))
     out[...] = out[...] + late.reshape(out.shape)
-    spectral_e(many, spectrum, coupled, coarse[1])
-    evaluate(k, "linear", spectrum, ((keep, damp), (damp, None)), out)
 
 
 def fast_per_device(counts, source, shift):
@@ -1443,7 +1449,7 @@
     dma = pltpu.SemaphoreType.DMA
     scratch += [dma((len(names) + 1,))] + [dma((1,))] * 4
     along, across = stages(counts)
-    scratch += TwoStage.semaphores(along) + [dma((1,))] * 4 + TwoStage.semaphores(across)
+    scratch += TwoStage.semaphores(along) + TwoStage.semaphores(across) * 2
     return pl.pallas_call(
         functools.partial(fast_kernel, names, counts),
         out_shape=jax.ShapeDtypeStruct(source.shape, jnp.float32),

time: 22.9 us -> 22 us (0.961)
  Pallas kernels: 21.5 us -> 20.5 us
    pallas_call x1, Pallas kernels: 21.5 us -> 20.5 us  [fast_per_device(): pl.pallas_call(functools.partial(fast_kernel, names, counts), out_shape=j...]
where the time goes in v4:
time: 22 us; the launch traced here: 21.8 us
  Pallas kernels  20.5 us (93%)
  local copies, waits for them, and re-layouts  0.66 us (3%)
  between operations  0.66 us (3%)
    pallas_call x1, Pallas kernels, fast_per_device(): pl.pallas_call(functools.partial(fast_kernel, names, counts), out_shape=j...  20.5 us
    unnamed x1, local copies, waits for them, and re-layouts  0.66 us

profile of v4, /device:TPU:0, one launch (start us, length us, event | category | flops | bytes accessed | tf_op | source)
XLA Modules:
  0.0 21.8 jit_solution(5368691518291951424)
XLA Ops:
  0.7 20.5 %shard_map.172 = f32[16,16,128]{2,1,0:T(8,128)S(1)} custom-call(bf16[256,384]{1,0:T(8,128)(2,1)} %constant.32.clone.refs_0_, bf16[192,256]{1,0:T(8,128)(2,1)} %constant.33.clone.refs_1_, bf16[512,128]{1,0:T(8,128)(2,1)} %constant.34.clone.refs_2_, f32[512,128]{1,0:T(8,128)} %constant.35.clone.refs_3_, f32[16,256]{1,0:T(8,128)} %constant.36.clone.refs_4_, ...), custom_call_target="tpu_custom_call" | custom-call | tf_op jit(solution)/shard_map/pallas_call | solution.py:1453
  21.2 0.7 %copy.21 = f32[16,16,128]{2,1,0:T(8,128)} copy(f32[16,16,128]{2,1,0:T(8,128)S(1)} %shard_map.172) | data formatting | bytes 262144

commit v5 on v4

--- a/solution.py
+++ b/solution.py
@@ -144,12 +144,12 @@
     )
 
 
-def loop(count, body):
+def loop(count, body, unroll=None):
     def step(i, carry):
         body(i)
         return carry
 
-    lax.fori_loop(0, count, step, 0, unroll=4 if count % 4 == 0 else 2)
+    lax.fori_loop(0, count, step, 0, unroll=unroll or (4 if count % 4 == 0 else 2))
 
 
 def close(ref):
@@ -965,8 +965,10 @@
                 self.send(arrived, arrived, second, len(self.near) + 1 + n)
             self.relay(arrived, arrived)
 
-    def rest(self):
-        for n, first in enumerate(((0, 0, 0), *self.near)):
+    def rest(self, which=None):
+        firsts = ((0, 0, 0), *self.near)
+        for n in range(len(firsts)) if which is None else which:
+            first = firsts[n]
             wait_for(self.landing.at[pl.ds(0, len(self.far))], self.arrived.at[len(self.near) + n])
             for second in self.far:
                 arrived = self.at(tuple(a + b for a, b in zip(first, second)))
@@ -992,11 +994,11 @@
 
 
 class Close:
-    def __init__(self, counts, near, block, landing, sems):
-        self.counts, self.near, self.block, self.landing = counts, near, block, landing
-        self.far = [((1, 0, 0), 1), ((counts[0] - 1, 0, 0), -1)] if counts[0] > 2 else [((1, 0, 0), 0)]
+    def __init__(self, counts, far, block, landing, sems):
+        self.counts, self.far, self.block, self.landing = counts, far, block, landing
+        self.near = [((1, 0, 0), 1), ((counts[0] - 1, 0, 0), -1)] if counts[0] > 2 else [((1, 0, 0), 0)]
         self.sent, self.arrived, self.relay_sent, self.relayed = sems
-        self.blocks = 2 * len(near) + 1
+        self.blocks = 2 * len(far) + 1
 
     def at(self, offset):
         source = shifted(position(), self.counts, tuple(-step for step in offset))
@@ -1011,24 +1013,29 @@
 
     def start(self):
         mine = self.at((0, 0, 0))
-        for n, offset in enumerate(self.near):
-            self.send(self.block, mine, offset, n)
-        for step, part in self.far:
-            self.send(piece(self.block, part), piece(mine, part), step, len(self.near))
+        for n, (step, part) in enumerate(self.near):
+            self.send(piece(self.block, part), piece(mine, part), step, n)
+        for step in self.far:
+            self.send(self.block, mine, step, len(self.near))
         self.relay(self.block, mine)
 
     def forward(self):
-        for n, first in enumerate(self.near):
-            arrived = self.at(first)
+        for n, (first, part) in enumerate(self.near):
+            arrived = piece(self.at(first), part)
             wait_for(arrived, self.arrived.at[n])
-            for step, part in self.far:
-                self.send(piece(arrived, part), piece(arrived, part), step, len(self.near) + 1 + n)
+            for step in self.far:
+                self.send(arrived, arrived, step, len(self.near) + 1 + n)
             self.relay(arrived, arrived)
 
     def rest(self):
-        for n, first in enumerate(((0, 0, 0), *self.near)):
-            wait_for(self.landing.at[0], self.arrived.at[len(self.near) + n])
-            for step, part in self.far:
+        count = len(self.far)
+        wait_for(self.landing.at[pl.ds(0, count)], self.arrived.at[len(self.near)])
+        for step in self.far:
+            self.relay(self.at(step), self.at(step))
+        for n, (first, part) in enumerate(self.near):
+            size = self.landing.shape[1] // (2 if part else 1)
+            wait_for(self.landing.at[pl.ds(0, count), pl.ds(0, size)], self.arrived.at[len(self.near) + 1 + n])
+            for step in self.far:
                 arrived = piece(self.at(tuple(a + b for a, b in zip(first, step))), part)
                 self.relay(arrived, arrived)
 
@@ -1134,14 +1141,14 @@
     def restrict(i):
         first[at(i), :] = sum(down[w] * spectrum[w] for w in blocks_of(spectrum, i))
 
-    loop(steps, restrict)
+    loop(steps, restrict, steps)
     second[...] = level2_full(k, few, first[...])
 
     def residue(i):
         u = second[at(i), :]
         first[at(i), :] = sum(pre[w] * (spectrum[w] - fine_q[w] * u) for w in blocks_of(spectrum, i))
 
-    loop(steps, residue)
+    loop(steps, residue, steps)
     third[...] = level2(k, few, first[...])
 
     def finish(i):
@@ -1155,7 +1162,7 @@
             total = pre[w] * value if total is None else total + pre[w] * value
         first[at(i), :] = total
 
-    loop(steps, finish)
+    loop(steps, finish, steps)
 
 
 def spectral_e(many, spectrum, coupled, e2):
@@ -1166,7 +1173,7 @@
         for w in blocks_of(spectrum, i):
             spectrum[w] = out_e[w] * e - out_g[w] * coupled[w]
 
-    loop(e2.shape[0] // 8, finish)
+    loop(e2.shape[0] // 8, finish, e2.shape[0] // 8)
 
 
 def unpack_centred(gathered, counts, g):
@@ -1290,7 +1297,7 @@
         beside = f[p] + f[p + 2] + around(f[p + 1])
         out[p] = damp * ((1.0 + keep) * source[p] + damp * beside[:rows, :lanes])
 
-    loop(source.shape[0], body)
+    loop(source.shape[0], body, source.shape[0])
 
 
 def fast_kernel(names, counts, *refs):
@@ -1340,7 +1347,7 @@
     exchange(counts, ([along_planes], [along_rows], [across]), faces_in, *face_sems[:2])
     gather_f = TwoStage(counts, along[::-1], across_all, block_f, landing_f, sems_f)
     gather_j = TwoStage(counts, across_all[::-1], along, block_j, landing_j, sems_j)
-    gather_f.start(along + across_all)
+    gather_f.start(along[::-1] + across_all)
     gather_f.own()
     own_planes[0] = source[0]
     own_planes[1] = source[b0 - 1]
@@ -1377,12 +1384,13 @@
     gather_f.forward(range(2, len(along)))
     mine = [[own.at[side] for side in range(2)] for own in (own_planes, own_rows, own_columns)]
     exchange(counts, mine, [halo.at[side] for halo in halos for side in range(2)], *face_sems[2:4])
+    close_h = Close(counts, across_all[::-1], block_h, landing_h, sems_h)
+    close_h.start()
     gather_j.start(along)
     gather_j.forward(range(len(across_all)))
-    close_h = Close(counts, across_all[::-1], block_h, landing_h, sems_h)
-    close_h.start()
-    gather_f.rest()
+    gather_f.rest(range(len(along)))
     close_h.forward()
+    gather_f.rest(range(len(along), len(along) + 1))
     for sem in face_sems[2:4]:
         wait_for(f.at[pl.ds(0, 2)], sem.at[0])
     f[...] = jnp.zeros_like(f)
@@ -1397,19 +1405,20 @@
     f[1 : b0 + 1, rows, pl.ds(b2, b2)] = turned.T.reshape(b0, b1, b2)
     keep = 1.0 - damp * diagonal
     own_sweep(f, source, keep, damp, out)
+    gather_j.rest()
     gather_f.end()
     for name in names:
         if name not in ("own", "early_rows", "early_lanes", "by_row", "by_lane", "eigen"):
             loads[name].wait()
     transform(k, counts, landing_f, g, spectrum)
     spectral_u(k, many, few, spectrum, coupled, coarse)
-    gather_j.rest()
+    gather_j.end()
     double = 2.0 * keep * damp
     square = damp * damp
     mix = ((keep * keep, double, square), (double, 2.0 * square, None), (square, None, None))
+    e2 = level2(k, few, transform2(k, counts, landing_j) - coarse[0][...])
     evaluate(k, "cubic", spectrum, mix, out)
-    gather_j.end()
-    coarse[1][...] = level2(k, few, transform2(k, counts, landing_j) - coarse[0][...])
+    coarse[1][...] = e2
     close_h.rest()
     spectral_e(many, spectrum, coupled, coarse[1])
     evaluate(k, "linear", spectrum, ((keep, damp), (damp, None)), out)
@@ -1449,7 +1458,7 @@
     dma = pltpu.SemaphoreType.DMA
     scratch += [dma((len(names) + 1,))] + [dma((1,))] * 4
     along, across = stages(counts)
-    scratch += TwoStage.semaphores(along) + TwoStage.semaphores(across) * 2
+    scratch += TwoStage.semaphores(along) * 2 + TwoStage.semaphores(across)
     return pl.pallas_call(
         functools.partial(fast_kernel, names, counts),
         out_shape=jax.ShapeDtypeStruct(source.shape, jnp.float32),

time: 22 us -> 20.6 us (0.936)
  Pallas kernels: 20.5 us -> 19.2 us
    pallas_call x1, Pallas kernels: 20.5 us -> 19.2 us  [fast_per_device(): pl.pallas_call(functools.partial(fast_kernel, names, counts), out_shape=j...]
where the time goes in v5:
time: 20.6 us; the launch traced here: 20.5 us
  Pallas kernels  19.2 us (93%)
  local copies, waits for them, and re-layouts  0.66 us (3%)
  between operations  0.66 us (3%)
    pallas_call x1, Pallas kernels, fast_per_device(): pl.pallas_call(functools.partial(fast_kernel, names, counts), out_shape=j...  19.2 us
    unnamed x1, local copies, waits for them, and re-layouts  0.66 us

profile of v5, /device:TPU:0, one launch (start us, length us, event | category | flops | bytes accessed | tf_op | source)
XLA Modules:
  0.0 20.5 jit_solution(10718554005248956476)
XLA Ops:
  0.7 19.2 %shard_map.172 = f32[16,16,128]{2,1,0:T(8,128)S(1)} custom-call(bf16[256,384]{1,0:T(8,128)(2,1)} %constant.32.clone.refs_0_, bf16[192,256]{1,0:T(8,128)(2,1)} %constant.33.clone.refs_1_, bf16[512,128]{1,0:T(8,128)(2,1)} %constant.34.clone.refs_2_, f32[512,128]{1,0:T(8,128)} %constant.35.clone.refs_3_, f32[16,256]{1,0:T(8,128)} %constant.36.clone.refs_4_, ...), custom_call_target="tpu_custom_call" | custom-call | tf_op jit(solution)/shard_map/pallas_call | solution.py:1462
  19.8 0.7 %copy.21 = f32[16,16,128]{2,1,0:T(8,128)} copy(f32[16,16,128]{2,1,0:T(8,128)S(1)} %shard_map.172) | data formatting | bytes 262144

commit v6 on v5

--- a/solution.py
+++ b/solution.py
@@ -1027,11 +1027,13 @@
                 self.send(arrived, arrived, step, len(self.near) + 1 + n)
             self.relay(arrived, arrived)
 
+    def rest_own(self):
+        wait_for(self.landing.at[pl.ds(0, len(self.far))], self.arrived.at[len(self.near)])
+        for step in self.far:
+            self.relay(self.at(step), self.at(step))
+
     def rest(self):
         count = len(self.far)
-        wait_for(self.landing.at[pl.ds(0, count)], self.arrived.at[len(self.near)])
-        for step in self.far:
-            self.relay(self.at(step), self.at(step))
         for n, (first, part) in enumerate(self.near):
             size = self.landing.shape[1] // (2 if part else 1)
             wait_for(self.landing.at[pl.ds(0, count), pl.ds(0, size)], self.arrived.at[len(self.near) + 1 + n])
@@ -1202,8 +1204,12 @@
     depth = half * m1
     for kind in range(2):
         rows = [g[p] - g[m0 - 1 - p] if kind else g[p] + g[m0 - 1 - p] for p in range(half)]
-        values = by_left(k["forward_rows"][kind], jnp.concatenate(rows, axis=0))
-        spectrum[kind * depth : (kind + 1) * depth, :] = by_right(values, k["forward_lanes"])
+        whole = jnp.concatenate(rows, axis=0)
+        part = depth // 2
+        for i in range(2):
+            values = by_left(k["forward_rows"][kind, i * part : (i + 1) * part], whole)
+            start = kind * depth + i * part
+            spectrum[start : start + part, :] = by_right(values, k["forward_lanes"])
 
 
 def transform2(k, counts, landing):
@@ -1232,8 +1238,9 @@
         values = by_left(k[kind + "_rows"][n], spectrum[n * depth : (n + 1) * depth, :])
         pieces = [values[i : i + half * rows] for i in range(0, values.shape[0], half * rows)]
         columns = [sum(c * pieces[i] for i, c in enumerate(line) if c is not None) for line in mix]
-        parts.append(by_right(jnp.concatenate(columns, axis=1), k[kind + "_lanes"]).reshape(half, rows, lanes))
-    even, odd = parts
+        parts.append(jnp.concatenate(columns, axis=1))
+    values = by_right(jnp.concatenate(parts, axis=0), k[kind + "_lanes"]).reshape(2, half, rows, lanes)
+    even, odd = values[0], values[1]
     for p in range(half):
         for index, value in ((half + p, even[p] + odd[p]), (half - 1 - p, even[p] - odd[p])):
             out[index] = out[index] + value
@@ -1382,15 +1389,16 @@
     block_h[end] = block_h[end] + damp * jnp.where(low, 0.0, from_planes[1][...])
 
     gather_f.forward(range(2, len(along)))
+    close_h = Close(counts, across_all[::-1], block_h, landing_h, sems_h)
+    close_h.start()
     mine = [[own.at[side] for side in range(2)] for own in (own_planes, own_rows, own_columns)]
     exchange(counts, mine, [halo.at[side] for halo in halos for side in range(2)], *face_sems[2:4])
-    close_h = Close(counts, across_all[::-1], block_h, landing_h, sems_h)
-    close_h.start()
     gather_j.start(along)
     gather_j.forward(range(len(across_all)))
     gather_f.rest(range(len(along)))
     close_h.forward()
     gather_f.rest(range(len(along), len(along) + 1))
+    close_h.rest_own()
     for sem in face_sems[2:4]:
         wait_for(f.at[pl.ds(0, 2)], sem.at[0])
     f[...] = jnp.zeros_like(f)

time: 20.6 us -> 20.3 us (0.985)
  Pallas kernels: 19.2 us -> 18.9 us
    pallas_call x1, Pallas kernels: 19.2 us -> 18.9 us  [fast_per_device(): pl.pallas_call(functools.partial(fast_kernel, names, counts), out_shape=j...]
where the time goes in v6:
time: 20.3 us; the launch traced here: 20.2 us
  Pallas kernels  18.9 us (93%)
  local copies, waits for them, and re-layouts  0.66 us (3%)
  between operations  0.66 us (3%)
    pallas_call x1, Pallas kernels, fast_per_device(): pl.pallas_call(functools.partial(fast_kernel, names, counts), out_shape=j...  18.9 us
    unnamed x1, local copies, waits for them, and re-layouts  0.66 us

profile of v6, /device:TPU:0, one launch (start us, length us, event | category | flops | bytes accessed | tf_op | source)
XLA Modules:
  0.0 20.2 jit_solution(12718722583177788744)
XLA Ops:
  0.7 18.9 %shard_map.172 = f32[16,16,128]{2,1,0:T(8,128)S(1)} custom-call(bf16[256,384]{1,0:T(8,128)(2,1)} %constant.32.clone.refs_0_, bf16[192,256]{1,0:T(8,128)(2,1)} %constant.33.clone.refs_1_, bf16[512,128]{1,0:T(8,128)(2,1)} %constant.34.clone.refs_2_, f32[512,128]{1,0:T(8,128)} %constant.35.clone.refs_3_, f32[16,256]{1,0:T(8,128)} %constant.36.clone.refs_4_, ...), custom_call_target="tpu_custom_call" | custom-call | tf_op jit(solution)/shard_map/pallas_call | solution.py:1470
  19.5 0.7 %copy.21 = f32[16,16,128]{2,1,0:T(8,128)} copy(f32[16,16,128]{2,1,0:T(8,128)S(1)} %shard_map.172) | data formatting | bytes 262144

commit v7 on v6

--- a/solution.py
+++ b/solution.py
@@ -934,7 +934,8 @@
     def __init__(self, counts, near, far, block, landing, sems):
         self.counts, self.near, self.far = counts, near, far
         self.block, self.landing = block, landing
-        self.sent, self.arrived, self.relay_sent, self.relayed = sems
+        self.sent, self.arrived, self.relayed = sems
+        self.relay_sent = self.sent
         self.count = 0
 
     def at(self, offset):
@@ -976,14 +977,13 @@
 
     def end(self):
         self.landing[slot(position(), self.counts)] = self.block[...]
-        wait_for(self.landing.at[pl.ds(0, self.count)], self.sent.at[0])
-        for sem in (self.relay_sent, self.relayed):
-            wait_for(self.landing.at[pl.ds(0, self.count + 1)], sem.at[0])
+        wait_for(self.landing.at[pl.ds(0, 2 * self.count + 1)], self.sent.at[0])
+        wait_for(self.landing.at[pl.ds(0, self.count + 1)], self.relayed.at[0])
 
     @staticmethod
     def semaphores(near):
         dma = pltpu.SemaphoreType.DMA
-        return [dma((1,)), dma((2 * len(near) + 1,)), dma((1,)), dma((1,))]
+        return [dma((1,)), dma((2 * len(near) + 1,)), dma((1,))]
 
 
 def piece(ref, part):
@@ -997,7 +997,8 @@
     def __init__(self, counts, far, block, landing, sems):
         self.counts, self.far, self.block, self.landing = counts, far, block, landing
         self.near = [((1, 0, 0), 1), ((counts[0] - 1, 0, 0), -1)] if counts[0] > 2 else [((1, 0, 0), 0)]
-        self.sent, self.arrived, self.relay_sent, self.relayed = sems
+        self.sent, self.arrived, self.relayed = sems
+        self.relay_sent = self.sent
         self.blocks = 2 * len(far) + 1
 
     def at(self, offset):
@@ -1043,9 +1044,8 @@
 
     def end(self):
         self.landing[slot(position(), self.counts)] = self.block[...]
-        wait_for(self.landing.at[pl.ds(0, self.blocks)], self.sent.at[0])
-        for sem in (self.relay_sent, self.relayed):
-            wait_for(self.landing.at[pl.ds(0, self.blocks + 1)], sem.at[0])
+        wait_for(self.landing.at[pl.ds(0, 2 * self.blocks + 1)], self.sent.at[0])
+        wait_for(self.landing.at[pl.ds(0, self.blocks + 1)], self.relayed.at[0])
 
 
 def exchange(counts, sent, received, send, recv):
@@ -1327,7 +1327,7 @@
     many, few, coarse = take(7), take(6), take(3)
     k["inverse"], g, near_h, spectrum, coupled, f = take(6)
     table_sems, *face_sems = take(5)
-    sems_f, sems_h, sems_j = take(4), take(4), take(4)
+    sems_f, sems_h, sems_j = take(3), take(3), take(3)
 
     shift = shift_ref[0]
     me = position()
@@ -1466,7 +1466,7 @@
     dma = pltpu.SemaphoreType.DMA
     scratch += [dma((len(names) + 1,))] + [dma((1,))] * 4
     along, across = stages(counts)
-    scratch += TwoStage.semaphores(along) * 2 + TwoStage.semaphores(across)
+    scratch += TwoStage.semaphores(along) + TwoStage.semaphores(along[:2]) + TwoStage.semaphores(across)
     return pl.pallas_call(
         functools.partial(fast_kernel, names, counts),
         out_shape=jax.ShapeDtypeStruct(source.shape, jnp.float32),

time: 20.3 us -> 20.3 us (level)
  no operation moved by 1% of the time
where the time goes in v7:
time: 20.3 us; the launch traced here: 20.1 us
  Pallas kernels  18.8 us (93%)
  local copies, waits for them, and re-layouts  0.66 us (3%)
  between operations  0.66 us (3%)
    pallas_call x1, Pallas kernels, fast_per_device(): pl.pallas_call(functools.partial(fast_kernel, names, counts), out_shape=j...  18.8 us
    unnamed x1, local copies, waits for them, and re-layouts  0.66 us

profile of v7, /device:TPU:0, one launch (start us, length us, event | category | flops | bytes accessed | tf_op | source)
XLA Modules:
  0.0 20.1 jit_solution(9098832866829671590)
XLA Ops:
  0.7 18.8 %shard_map.172 = f32[16,16,128]{2,1,0:T(8,128)S(1)} custom-call(bf16[256,384]{1,0:T(8,128)(2,1)} %constant.32.clone.refs_0_, bf16[192,256]{1,0:T(8,128)(2,1)} %constant.33.clone.refs_1_, bf16[512,128]{1,0:T(8,128)(2,1)} %constant.34.clone.refs_2_, f32[512,128]{1,0:T(8,128)} %constant.35.clone.refs_3_, f32[16,256]{1,0:T(8,128)} %constant.36.clone.refs_4_, ...), custom_call_target="tpu_custom_call" | custom-call | tf_op jit(solution)/shard_map/pallas_call | solution.py:1470
  19.5 0.7 %copy.21 = f32[16,16,128]{2,1,0:T(8,128)} copy(f32[16,16,128]{2,1,0:T(8,128)S(1)} %shard_map.172) | data formatting | bytes 262144
